TPU v7x, 32 devices: a whole 2x2x4 slice. The times are simulated.
32 devices in a mesh: exp: 8 (over z, x), dat: 4 (over y, core).
Axes of the slice: x: 2, y: 2, z: 4, core: 2. Of those that a mesh axis runs over, the one named last changes fastest.
Arguments:
- tokens: bfloat16 [4096, 1024], P(('exp', 'dat')), may hold values from -6 to 6
- norm_gain: float32 [1024], replicated, may hold values from 0.25 to 1.75
- router_weight: bfloat16 [1024, 32], P(None, 'exp'), may hold values from -0.1875 to 0.1875
- inner_weight: bfloat16 [32, 1024, 4096], P('exp', None, 'dat'), may hold values from -0.1875 to 0.1875
- outer_weight: bfloat16 [32, 4096, 1024], P('exp', 'dat'), may hold values from -0.09375 to 0.09375
- slot_tokens: int32 [32, 256], P('exp', 'dat'), may hold values from 0 to 4095, as said below
- slot_ids: int32 [4096, 2], P(('exp', 'dat')), may hold values from 0 to 8191, as said below
Outputs:
- mixed: bfloat16 [4096, 1024], P(('exp', 'dat'))
Inputs may be any that keep to these rules, and one draw needn't show every extreme that they name: `slot_tokens`: column c of an expert names only tokens of the devices whose dat index is c // 64; one expert names no token twice. The 256 slots of the experts of one exp index in one dat group name tokens of any one device at most 96 times, exactly 96 times for some devices, and no times for some. Every token is named by exactly 2 slots. slot_ids[t] holds the two slots e * 256 + c with slot_tokens[e, c] = t, the smaller first.
All inputs are finite; a program needn't handle non-finite values.
Results may differ from a plain program's by a relative error of at most 0.0085.
Values may be sent and summed in bfloat16 or wider, within the bound.
A program may use at most 64 MiB of HBM per device.

v0:
```python
import jax
import jax.numpy as jnp
from jax import lax
from jax.experimental import pallas as pl
from jax.experimental.pallas import tpu as pltpu
from jax.sharding import PartitionSpec as P

EPSILON = 1e-06


def normalize(tokens, norm_gain):
    values = tokens.astype(jnp.float32)
    scale = lax.rsqrt(jnp.mean(values * values, axis=-1, keepdims=True) + EPSILON)
    return (values * scale * norm_gain).astype(jnp.bfloat16)


def owner_places(slot_ids, experts_dev, capacity, bucket):
    flat_ids = slot_ids.reshape(-1)
    source = flat_ids // capacity // experts_dev
    before = (source[:, None] == source[None, :]) & (flat_ids[None, :] < flat_ids[:, None])
    ranks_in = jnp.sum(before.astype(jnp.int32), axis=1)
    return (source * bucket + ranks_in).reshape(slot_ids.shape)


def expert_places(token_ids, slot_keys, tok_rows, dat_count, bucket):
    owner_of = token_ids // (tok_rows * dat_count)
    before = (owner_of[:, None] == owner_of[None, :]) & (slot_keys[None, :] < slot_keys[:, None])
    ranks_in = jnp.sum(before.astype(jnp.int32), axis=1)
    return owner_of * bucket + ranks_in


def body(tokens, norm_gain, router_weight, inner_weight, outer_weight, slot_tokens, slot_ids):
    exp_count = lax.axis_size("exp")
    dat_count = lax.axis_size("dat")
    tok_rows, width = tokens.shape
    experts_dev, cap_dev = slot_tokens.shape
    bucket = 6 * tok_rows // exp_count
    normed = normalize(tokens, norm_gain)
    picked = slot_tokens.T.reshape(-1)
    expert_iota = lax.broadcasted_iota(jnp.int32, (cap_dev, experts_dev), 1)
    column_iota = lax.broadcasted_iota(jnp.int32, (cap_dev, experts_dev), 0)
    slot_keys = (expert_iota * cap_dev + column_iota).reshape(-1)
    senders = expert_places(picked, slot_keys, tok_rows, dat_count, bucket)
    receivers = owner_places(slot_ids, experts_dev, cap_dev * dat_count, bucket)
    lookup = jnp.any(
        lax.broadcasted_iota(jnp.int32, (exp_count * bucket, 1, 1), 0) == receivers[None], axis=2
    )
    outgoing = jnp.dot(lookup.astype(jnp.bfloat16), normed, preferred_element_type=jnp.float32)
    outgoing = outgoing.astype(jnp.bfloat16).reshape(exp_count, bucket, width)
    arrived = lax.all_to_all(outgoing, "exp", split_axis=0, concat_axis=0, tiled=True).reshape(
        exp_count * bucket, width
    )
    gathered_rows = jnp.take(arrived, senders, axis=0)
    gathered_rows = gathered_rows.reshape(cap_dev, experts_dev, width)
    gate_score = jax.nn.sigmoid(
        jnp.einsum("ced,de->ce", gathered_rows, router_weight, preferred_element_type=jnp.float32)
    )
    inner = jnp.einsum(
        "ced,edf->cef",
        lax.all_gather(gathered_rows, "dat", axis=0, tiled=True),
        inner_weight,
        preferred_element_type=jnp.float32,
    )
    hidden = jax.nn.relu(inner).astype(jnp.bfloat16)
    expert_out = lax.psum_scatter(
        jnp.einsum("cef,efd->ced", hidden, outer_weight, preferred_element_type=jnp.float32).astype(
            jnp.bfloat16
        ),
        "dat",
        scatter_dimension=0,
        tiled=True,
    ).astype(jnp.float32)
    weighted = (gate_score[:, :, None] * expert_out).astype(jnp.bfloat16).reshape(-1, width)
    placing = lax.broadcasted_iota(jnp.int32, (exp_count * bucket, 1), 0) == senders[None, :]
    returning = jnp.dot(placing.astype(jnp.bfloat16), weighted, preferred_element_type=jnp.float32)
    returning = returning.astype(jnp.bfloat16).reshape(exp_count, bucket, width)
    came_back = lax.all_to_all(returning, "exp", split_axis=0, concat_axis=0, tiled=True).reshape(
        exp_count * bucket, width
    )
    combine_table = jnp.sum(
        (
            lax.broadcasted_iota(jnp.int32, (1, 1, exp_count * bucket), 2) == receivers[:, :, None]
        ).astype(jnp.float32),
        axis=1,
    )
    combined = jnp.dot(
        combine_table.astype(jnp.bfloat16), came_back, preferred_element_type=jnp.float32
    )
    return (tokens.astype(jnp.float32) + combined).astype(jnp.bfloat16)


MESH = pl.DeviceIdType.MESH
PAIR = 2
CHUNK = 256
GROUP = 256


def moe_kernel(
    tokens_ref, gain_ref, router_ref, ids_ref, inner_hbm, outer_hbm, out_ref,
    inner_v, outer_v, ids_far, pick, place, blocks, own_part, far_send, far_recv,
    rows, sums, hidden, gate, parts, core_recv, y_send, y_recv, kept, weighted, x_recv,
    dense, up_send, up_recv, down_send, down_recv,
    w_sem, ids_sem, zu_sem, zd_sem, x_sem, y_sem, c_sem, cr_sem,
    rc_sem, ry_sem, rx_sem, ru_sem, rd_sem,
):
    chunks, lines, tok_rows, wide = blocks.shape
    experts_dev = inner_v.shape[0]
    slots = weighted.shape[1]
    groups, span = rows.shape[0], rows.shape[3]
    per = span // wide
    cap_dev = slots // experts_dev
    exp = lax.axis_index("exp")
    dat = lax.axis_index("dat")
    dat_count = lax.axis_size("dat")
    z, x = exp // PAIR, exp % PAIR
    y, c = dat // PAIR, dat % PAIR
    up = (exp + PAIR, dat)
    down = (exp - PAIR, dat)
    x_peer = (exp + 1 - 2 * x, dat)
    y_peer = (exp, dat + PAIR - 2 * PAIR * y)
    c_peer = (exp, dat + 1 - 2 * c)
    has_up = z + 1 < lines
    has_down = z > 0
    sent = []

    def copy_to(src, dst, sems, where, peer):
        return pltpu.make_async_remote_copy(
            src_ref=src, dst_ref=dst, send_sem=sems.at[(0,) + where],
            recv_sem=sems.at[(1,) + where], device_id=peer, device_id_type=MESH,
        )

    def send(copy, cond=None):
        sent.append((copy, cond))
        if cond is None:
            copy.start()
        else:
            pl.when(cond)(copy.start)

    loads = []
    for e in range(experts_dev):
        loads.append(pltpu.make_async_copy(inner_hbm.at[e], inner_v.at[e], w_sem.at[0, e]))
    for e in range(experts_dev):
        loads.append(pltpu.make_async_copy(outer_hbm.at[e], outer_v.at[e], w_sem.at[1, e]))
    for load in loads:
        load.start()

    barrier = pltpu.get_barrier_semaphore()
    for peer in (x_peer, y_peer, c_peer):
        pl.semaphore_signal(barrier, inc=1, device_id=peer, device_id_type=MESH)

    @pl.when(has_up)
    def _():
        pl.semaphore_signal(barrier, inc=1, device_id=up, device_id_type=MESH)

    @pl.when(has_down)
    def _():
        pl.semaphore_signal(barrier, inc=1, device_id=down, device_id_type=MESH)

    values = tokens_ref[...].astype(jnp.float32)
    scale = lax.rsqrt(jnp.mean(values * values, axis=-1, keepdims=True) + EPSILON)
    normed = (values * scale * gain_ref[...]).astype(jnp.bfloat16)
    for j in range(chunks):
        blocks[j, z] = normed[:, j * wide : (j + 1) * wide]

    pl.semaphore_wait(barrier, 3 + has_up.astype(jnp.int32) + has_down.astype(jnp.int32))

    ids_copy = copy_to(ids_ref, ids_far, ids_sem, (), x_peer)

    def one_hots(side, ids):
        for s in range(lines):
            base = ((s * PAIR + x) * dat_count + dat) * tok_rows
            local = lax.broadcasted_iota(jnp.int32, (tok_rows, slots), 0) + base
            all_ids = jnp.concatenate([ids[e : e + 1, :] for e in range(experts_dev)], axis=1)
            hot = (all_ids == local).astype(jnp.float32)
            place[side, s * tok_rows : (s + 1) * tok_rows, :] = hot.astype(jnp.bfloat16)
            pick[side, :, s * tok_rows : (s + 1) * tok_rows] = hot.T.astype(jnp.bfloat16)

    def own_rows(j, of_dat):
        first = (j % per) * wide
        at = pl.ds(pl.multiple_of(of_dat * cap_dev, cap_dev), cap_dev)
        return rows.at[j // per, :, at, first : first + wide]

    def first_product(g):
        if g == 0:
            for e in range(experts_dev):
                loads[e].wait()

        @pl.loop(0, experts_dev, unroll=True)
        def _(e):
            total = jnp.dot(
                rows[g, e], inner_v[e, g * span : (g + 1) * span, :], preferred_element_type=jnp.float32
            )
            if g > 0:
                total += sums[e]
            if g + 1 < groups:
                sums[e] = total
            else:
                hidden[e] = jnp.maximum(total, 0.0).astype(jnp.bfloat16)

    dat_y = dat + PAIR - 2 * PAIR * y
    dat_c = dat + 1 - 2 * c
    dat_yc = dat_y + 1 - 2 * c

    for t in range(chunks + lines + 3):
        if t < chunks:
            send(copy_to(blocks.at[t, z], blocks.at[t, z], zu_sem, (t, z), up), has_up)
            send(copy_to(blocks.at[t, z], blocks.at[t, z], zd_sem, (t, z), down), has_down)
        if t == 0:
            send(ids_copy)
            one_hots(0, ids_ref)
        if t == 1:
            ids_copy.wait_recv()
            one_hots(1, ids_far)
        for k in range(1, lines):
            j = t - k
            if 0 <= j < chunks:
                low, high = z - k, z + k
                from_low = copy_to(blocks.at[j, low], blocks.at[j, low], zu_sem, (j, low), up)
                from_high = copy_to(blocks.at[j, high], blocks.at[j, high], zd_sem, (j, high), down)
                pl.when(low >= 0)(from_low.wait_recv)
                if k + 1 < lines:
                    send(from_low, (low >= 0) & has_up)
                pl.when(high < lines)(from_high.wait_recv)
                if k + 1 < lines:
                    send(from_high, (high < lines) & has_down)
        j = t - (lines - 1)
        if 0 <= j < chunks:
            found = blocks[j].reshape(lines * tok_rows, wide)
            far_send[j] = jnp.dot(pick[1], found, preferred_element_type=jnp.float32).astype(jnp.bfloat16)
            send(copy_to(far_send.at[j], far_recv.at[j], x_sem, (j,), x_peer))
            own_part[j] = jnp.dot(pick[0], found, preferred_element_type=jnp.float32)
        j = t - lines
        if 0 <= j < chunks:
            copy_to(far_send.at[j], far_recv.at[j], x_sem, (j,), x_peer).wait_recv()
            merged = (own_part[j] + far_recv[j].astype(jnp.float32)).astype(jnp.bfloat16)
            own_rows(j, dat)[...] = merged.reshape(experts_dev, cap_dev, wide)
            send(copy_to(own_rows(j, dat), own_rows(j, dat), y_sem, (j,), y_peer))
            send(copy_to(own_rows(j, dat), own_rows(j, dat), c_sem, (j,), c_peer))
            score = lax.dot_general(
                merged, router_ref[:, j * wide : (j + 1) * wide], (((1,), (1,)), ((), ())),
                preferred_element_type=jnp.float32,
            )
            row_id = lax.broadcasted_iota(jnp.int32, score.shape, 0)
            first = lax.broadcasted_iota(jnp.int32, score.shape, 1) * cap_dev
            mine = (row_id >= first) & (row_id < first + cap_dev)
            score = jnp.sum(jnp.where(mine, score, 0.0), axis=1, keepdims=True)
            gate[...] = score if j == 0 else gate[...] + score
        j = t - lines - 1
        if 0 <= j < chunks:
            copy_to(own_rows(j, dat_y), own_rows(j, dat_y), y_sem, (j,), y_peer).wait_recv()
            send(copy_to(own_rows(j, dat_y), own_rows(j, dat_y), cr_sem, (j,), c_peer))
        j = t - lines - 2
        if 0 <= j < chunks:
            copy_to(own_rows(j, dat_c), own_rows(j, dat_c), c_sem, (j,), c_peer).wait_recv()
            copy_to(own_rows(j, dat_yc), own_rows(j, dat_yc), cr_sem, (j,), c_peer).wait_recv()
            if (j + 1) % per == 0:
                first_product(j // per)
    gate[...] = jax.nn.sigmoid(gate[...])
    for e in range(experts_dev):
        loads[experts_dev + e].wait()

    def block(s):
        return slice(s * tok_rows, (s + 1) * tok_rows)

    for t in range(chunks + 4 + lines):
        j = t
        if j < chunks:
            if j % per == 0:

                @pl.loop(0, experts_dev, unroll=True)
                def _(e, j=j):
                    part = jnp.dot(
                        hidden[e], outer_v[e, :, j * wide : j * wide + span], preferred_element_type=jnp.float32
                    ).astype(jnp.bfloat16)
                    for d in range(PAIR * PAIR):
                        for k in range(per):
                            parts[j + k, d // PAIR, d % PAIR, e] = part[
                                d * cap_dev : (d + 1) * cap_dev, k * wide : (k + 1) * wide
                            ]

            send(copy_to(parts.at[j, :, 1 - c], core_recv.at[j], rc_sem, (j,), c_peer))
        j = t - 1
        if 0 <= j < chunks:
            copy_to(parts.at[j, :, 1 - c], core_recv.at[j], rc_sem, (j,), c_peer).wait_recv()
            theirs = parts[j, 1 - y, c].astype(jnp.float32) + core_recv[j, 1 - y].astype(jnp.float32)
            y_send[j] = theirs.astype(jnp.bfloat16).reshape(slots, wide)
            send(copy_to(y_send.at[j], y_recv.at[j], ry_sem, (j,), y_peer))
            ours = parts[j, y, c].astype(jnp.float32) + core_recv[j, y].astype(jnp.float32)
            kept[j] = ours.reshape(slots, wide)
        j = t - 2
        if 0 <= j < chunks:
            copy_to(y_send.at[j], y_recv.at[j], ry_sem, (j,), y_peer).wait_recv()
            summed = kept[j] + y_recv[j].astype(jnp.float32)
            weighted[j] = (gate[...] * summed).astype(jnp.bfloat16)
            send(copy_to(weighted.at[j], x_recv.at[j], rx_sem, (j,), x_peer))
        j = t - 3
        if 0 <= j < chunks:
            copy_to(weighted.at[j], x_recv.at[j], rx_sem, (j,), x_peer).wait_recv()
            spread = jnp.dot(place[0], weighted[j], preferred_element_type=jnp.float32)
            spread += jnp.dot(place[1], x_recv[j], preferred_element_type=jnp.float32)
            dense[j] = spread
        for s in range(lines):
            j = t - 3 - s
            if not 0 <= j < chunks:
                continue
            for dest in range(lines - 1, s, -1):
                here = z == s
                go = copy_to(up_send.at[j, dest], up_recv.at[j, dest], ru_sem, (j, dest), up)

                @pl.when(here)
                def _(j=j, dest=dest, s=s, go=go):
                    total = dense[j, block(dest), :]
                    if s > 0:
                        go.wait_recv()
                        total += up_recv[j, dest].astype(jnp.float32)
                    up_send[j, dest] = total.astype(jnp.bfloat16)

                send(go, here)
            top = lines - 1 - s
            for dest in range(top):
                here = z == top
                go = copy_to(down_send.at[j, dest], down_recv.at[j, dest], rd_sem, (j, dest), down)

                @pl.when(here)
                def _(j=j, dest=dest, top=top, go=go):
                    total = dense[j, block(dest), :]
                    if top < lines - 1:
                        go.wait_recv()
                        total += down_recv[j, dest].astype(jnp.float32)
                    down_send[j, dest] = total.astype(jnp.bfloat16)

                send(go, here)
        j = t - 3 - lines
        if 0 <= j < chunks:
            for s in range(lines):

                @pl.when(z == s)
                def _(j=j, s=s):
                    cols = slice(j * wide, (j + 1) * wide)
                    total = dense[j, block(s), :]
                    if s > 0:
                        copy_to(up_send.at[j, s], up_recv.at[j, s], ru_sem, (j, s), up).wait_recv()
                        total += up_recv[j, s].astype(jnp.float32)
                    if s < lines - 1:
                        copy_to(down_send.at[j, s], down_recv.at[j, s], rd_sem, (j, s), down).wait_recv()
                        total += down_recv[j, s].astype(jnp.float32)
                    out_ref[:, cols] = (tokens_ref[:, cols].astype(jnp.float32) + total).astype(jnp.bfloat16)

    for copy, cond in sent:
        if cond is None:
            copy.wait_send()
        else:
            pl.when(cond)(copy.wait_send)


def kernel_body(tokens, norm_gain, router_weight, inner_weight, outer_weight, slot_tokens, slot_ids):
    del slot_ids
    tok_rows, width = tokens.shape
    experts_dev, cap_dev = slot_tokens.shape
    units = inner_weight.shape[2]
    lines = lax.axis_size("exp") // PAIR
    dat_count = lax.axis_size("dat")
    slots = experts_dev * cap_dev
    chunks = width // CHUNK
    bf16, f32 = jnp.bfloat16, jnp.float32
    vmem = pl.BlockSpec(memory_space=pltpu.VMEM)
    hbm = pl.BlockSpec(memory_space=pl.ANY)
    dma = pltpu.SemaphoreType.DMA
    return pl.pallas_call(
        moe_kernel,
        out_shape=jax.ShapeDtypeStruct((tok_rows, width), bf16),
        in_specs=[vmem, vmem, vmem, vmem, hbm, hbm],
        out_specs=vmem,
        scratch_shapes=[
            pltpu.VMEM((experts_dev, width, units), bf16),
            pltpu.VMEM((experts_dev, units, width), bf16),
            pltpu.VMEM((experts_dev, cap_dev), jnp.int32),
            pltpu.VMEM((2, slots, lines * tok_rows), bf16),
            pltpu.VMEM((2, lines * tok_rows, slots), bf16),
            pltpu.VMEM((chunks, lines, tok_rows, CHUNK), bf16),
            pltpu.VMEM((chunks, slots, CHUNK), f32),
            pltpu.VMEM((chunks, slots, CHUNK), bf16),
            pltpu.VMEM((chunks, slots, CHUNK), bf16),
            pltpu.VMEM((width // GROUP, experts_dev, dat_count * cap_dev, GROUP), bf16),
            pltpu.VMEM((experts_dev, dat_count * cap_dev, units), f32),
            pltpu.VMEM((experts_dev, dat_count * cap_dev, units), bf16),
            pltpu.VMEM((slots, 1), f32),
            pltpu.VMEM((chunks, PAIR, PAIR, experts_dev, cap_dev, CHUNK), bf16),
            pltpu.VMEM((chunks, PAIR, experts_dev, cap_dev, CHUNK), bf16),
            pltpu.VMEM((chunks, slots, CHUNK), bf16),
            pltpu.VMEM((chunks, slots, CHUNK), bf16),
            pltpu.VMEM((chunks, slots, CHUNK), f32),
            pltpu.VMEM((chunks, slots, CHUNK), bf16),
            pltpu.VMEM((chunks, slots, CHUNK), bf16),
            pltpu.VMEM((chunks, lines * tok_rows, CHUNK), f32),
            pltpu.VMEM((chunks, lines, tok_rows, CHUNK), bf16),
            pltpu.VMEM((chunks, lines, tok_rows, CHUNK), bf16),
            pltpu.VMEM((chunks, lines, tok_rows, CHUNK), bf16),
            pltpu.VMEM((chunks, lines, tok_rows, CHUNK), bf16),
            dma((2, experts_dev)),
            dma((2,)),
            dma((2, chunks, lines)),
            dma((2, chunks, lines)),
            dma((2, chunks)),
            dma((2, chunks)),
            dma((2, chunks)),
            dma((2, chunks)),
            dma((2, chunks)),
            dma((2, chunks)),
            dma((2, chunks)),
            dma((2, chunks, lines)),
            dma((2, chunks, lines)),
        ],
        compiler_params=pltpu.CompilerParams(
            collective_id=0, has_side_effects=True, vmem_limit_bytes=60 * 1024 * 1024
        ),
    )(tokens, norm_gain.reshape(1, width), router_weight.T, slot_tokens, inner_weight, outer_weight)


def solution(mesh):
    chosen = kernel_body if mesh.shape["dat"] == PAIR * PAIR else body
    in_specs = (
        P(("exp", "dat"), None),
        P(),
        P(None, "exp"),
        P("exp", None, "dat"),
        P("exp", "dat", None),
        P("exp", "dat"),
        P(("exp", "dat"), None),
    )
    out_specs = P(("exp", "dat"), None)
    return jax.shard_map(chosen, mesh=mesh, in_specs=in_specs, out_specs=out_specs, check_vma=False)
```

profile of v0, /device:TPU:0, one launch (start us, length us, event | category | flops | bytes accessed | tf_op | source)
XLA Modules:
  0.0 77.3 jit_solution(5091043987613149511)
XLA Ops:
  0.0 75.6 %shard_map.64 = bf16[128,1024]{1,0:T(8,128)(2,1)} custom-call(bf16[128,1024]{1,0:T(8,128)(2,1)} %tokens_ref.1, f32[1,1024]{1,0:T(1,128)} %bitcast.3, bf16[4,1024]{1,0:T(4,128)(2,1)} %bitcast.2, s32[4,64]{1,0:T(4,128)} %ids_ref.1, bf16[4,1024,1024]{2,1,0:T(8,128)(2,1)} %inner_hbm.1, bf16[4,1024,1024]{2,1,0:T(8,128)(2,1)} %outer_hbm.1), custom_call_target="tpu_custom_call" | custom-call | tf_op jit(solution)/shard_map/pallas_call | solution.py:369
  75.6 1.7 %copy.8 = bf16[128,1024]{1,0:T(8,128)(2,1)} copy(bf16[128,1024]{1,0:T(8,128)(2,1)} %shard_map.64) | data formatting | bytes 524288
where the time goes:
time: 77.4 us; the launch traced here: 77.3 us
  Pallas kernels  75.6 us (98%)
  local copies, waits for them, and re-layouts  1.67 us (2%)
    pallas_call x1, Pallas kernels, kernel_body(): pl.pallas_call(moe_kernel, out_shape=jax.ShapeDtypeStruct((tok_rows, widt...  75.6 us
    unnamed x1, local copies, waits for them, and re-layouts  1.67 us

commit v1 on v0

v1 whole, which is shorter than its diff:
```python
import jax
import jax.numpy as jnp
from jax import lax
from jax.experimental import pallas as pl
from jax.experimental.pallas import tpu as pltpu
from jax.sharding import PartitionSpec as P

EPSILON = 1e-06


def normalize(tokens, norm_gain):
    values = tokens.astype(jnp.float32)
    scale = lax.rsqrt(jnp.mean(values * values, axis=-1, keepdims=True) + EPSILON)
    return (values * scale * norm_gain).astype(jnp.bfloat16)


def owner_places(slot_ids, experts_dev, capacity, bucket):
    flat_ids = slot_ids.reshape(-1)
    source = flat_ids // capacity // experts_dev
    before = (source[:, None] == source[None, :]) & (flat_ids[None, :] < flat_ids[:, None])
    ranks_in = jnp.sum(before.astype(jnp.int32), axis=1)
    return (source * bucket + ranks_in).reshape(slot_ids.shape)


def expert_places(token_ids, slot_keys, tok_rows, dat_count, bucket):
    owner_of = token_ids // (tok_rows * dat_count)
    before = (owner_of[:, None] == owner_of[None, :]) & (slot_keys[None, :] < slot_keys[:, None])
    ranks_in = jnp.sum(before.astype(jnp.int32), axis=1)
    return owner_of * bucket + ranks_in


def body(tokens, norm_gain, router_weight, inner_weight, outer_weight, slot_tokens, slot_ids):
    exp_count = lax.axis_size("exp")
    dat_count = lax.axis_size("dat")
    tok_rows, width = tokens.shape
    experts_dev, cap_dev = slot_tokens.shape
    bucket = 6 * tok_rows // exp_count
    normed = normalize(tokens, norm_gain)
    picked = slot_tokens.T.reshape(-1)
    expert_iota = lax.broadcasted_iota(jnp.int32, (cap_dev, experts_dev), 1)
    column_iota = lax.broadcasted_iota(jnp.int32, (cap_dev, experts_dev), 0)
    slot_keys = (expert_iota * cap_dev + column_iota).reshape(-1)
    senders = expert_places(picked, slot_keys, tok_rows, dat_count, bucket)
    receivers = owner_places(slot_ids, experts_dev, cap_dev * dat_count, bucket)
    lookup = jnp.any(
        lax.broadcasted_iota(jnp.int32, (exp_count * bucket, 1, 1), 0) == receivers[None], axis=2
    )
    outgoing = jnp.dot(lookup.astype(jnp.bfloat16), normed, preferred_element_type=jnp.float32)
    outgoing = outgoing.astype(jnp.bfloat16).reshape(exp_count, bucket, width)
    arrived = lax.all_to_all(outgoing, "exp", split_axis=0, concat_axis=0, tiled=True).reshape(
        exp_count * bucket, width
    )
    gathered_rows = jnp.take(arrived, senders, axis=0)
    gathered_rows = gathered_rows.reshape(cap_dev, experts_dev, width)
    gate_score = jax.nn.sigmoid(
        jnp.einsum("ced,de->ce", gathered_rows, router_weight, preferred_element_type=jnp.float32)
    )
    inner = jnp.einsum(
        "ced,edf->cef",
        lax.all_gather(gathered_rows, "dat", axis=0, tiled=True),
        inner_weight,
        preferred_element_type=jnp.float32,
    )
    hidden = jax.nn.relu(inner).astype(jnp.bfloat16)
    expert_out = lax.psum_scatter(
        jnp.einsum("cef,efd->ced", hidden, outer_weight, preferred_element_type=jnp.float32).astype(
            jnp.bfloat16
        ),
        "dat",
        scatter_dimension=0,
        tiled=True,
    ).astype(jnp.float32)
    weighted = (gate_score[:, :, None] * expert_out).astype(jnp.bfloat16).reshape(-1, width)
    placing = lax.broadcasted_iota(jnp.int32, (exp_count * bucket, 1), 0) == senders[None, :]
    returning = jnp.dot(placing.astype(jnp.bfloat16), weighted, preferred_element_type=jnp.float32)
    returning = returning.astype(jnp.bfloat16).reshape(exp_count, bucket, width)
    came_back = lax.all_to_all(returning, "exp", split_axis=0, concat_axis=0, tiled=True).reshape(
        exp_count * bucket, width
    )
    combine_table = jnp.sum(
        (
            lax.broadcasted_iota(jnp.int32, (1, 1, exp_count * bucket), 2) == receivers[:, :, None]
        ).astype(jnp.float32),
        axis=1,
    )
    combined = jnp.dot(
        combine_table.astype(jnp.bfloat16), came_back, preferred_element_type=jnp.float32
    )
    return (tokens.astype(jnp.float32) + combined).astype(jnp.bfloat16)


MESH = pl.DeviceIdType.MESH
PAIR = 2
LINE = 4
LANES = 128
PARTS = 2


def moe_kernel(
    tokens_ref, gain_ref, router_ref, ids_ref, inner_hbm, outer_hbm, out_ref,
    inner_v, outer_v, ids_all, pick_own, place_own, pick_far, place_far,
    blocks, cross, pick_send, pick_recv, swap_send, rows, sums, hidden, gate,
    parts, core_recv, y_send, y_recv, kept, give, slots_v, raw, dense, dest_send, dest_recv,
    last_send, last_recv, last_own,
    w_sem, ids_sem, x_sem, near_sem, far_sem, pick_sem, swap_sem, y_sem, c_sem, cr_sem,
    rc_sem, ry_sem, rx_sem, raw_sem, dest_sem, last_sem,
):
    chunks = blocks.shape[0]
    tok_rows = tokens_ref.shape[0]
    experts_dev, cap_dev = ids_ref.shape
    slots = experts_dev * cap_dev
    both = PAIR * tok_rows
    wide = PAIR * LANES
    pair_e = experts_dev // PARTS
    bf16, f32 = jnp.bfloat16, jnp.float32
    exp = lax.axis_index("exp")
    dat = lax.axis_index("dat")
    dat_count = lax.axis_size("dat")
    z, x = exp // PAIR, exp % PAIR
    y, c = dat // PAIR, dat % PAIR
    half = z // PAIR
    spot = z + half * (LINE - 1 - 2 * z)
    is_end = spot == 0
    is_inner = spot == 1

    def line_z(q):
        return q + half * (LINE - 1 - 2 * q)

    near = (line_z(1 - spot) * PAIR + x, dat)
    far_inner = (line_z(2) * PAIR + x, dat)
    far_end = (line_z(3) * PAIR + x, dat)
    x_peer = (exp + 1 - 2 * x, dat)
    y_peer = (exp, dat + PAIR - 2 * PAIR * y)
    c_peer = (exp, dat + 1 - 2 * c)
    sent = []

    def copy_to(src, dst, sems, where, peer):
        return pltpu.make_async_remote_copy(
            src_ref=src, dst_ref=dst, send_sem=sems.at[(0,) + where],
            recv_sem=sems.at[(1,) + where], device_id=peer, device_id_type=MESH,
        )

    def send(copy, cond=None):
        sent.append((copy, cond))
        if cond is None:
            copy.start()
        else:
            pl.when(cond)(copy.start)

    loads = []
    for e in range(experts_dev):
        loads.append(pltpu.make_async_copy(inner_hbm.at[e], inner_v.at[e], w_sem.at[0, e]))
    for e in range(experts_dev):
        loads.append(pltpu.make_async_copy(outer_hbm.at[e], outer_v.at[e], w_sem.at[1, e]))

    barrier = pltpu.get_barrier_semaphore()
    for peer in (near, far_inner, x_peer, y_peer, c_peer):
        pl.semaphore_signal(barrier, inc=1, device_id=peer, device_id_type=MESH)

    @pl.when(is_inner)
    def _():
        pl.semaphore_signal(barrier, inc=1, device_id=far_end, device_id_type=MESH)

    for load in loads:
        load.start()

    values = tokens_ref[...].astype(f32)
    scale = lax.rsqrt(jnp.mean(values * values, axis=-1, keepdims=True) + EPSILON)
    normed = values * scale * gain_ref[...]

    def split(value):
        low, high = value[..., :LANES], value[..., LANES:]
        return jnp.where(x == 0, low, high), jnp.where(x == 0, high, low)

    for k in range(chunks):
        own, other = split(normed[:, k * wide : (k + 1) * wide])
        blocks[k, spot, 0] = own.astype(bf16)
        cross[k] = other.astype(bf16)

    def one_hots(ids, side, pick, place, first):
        row = jnp.concatenate([ids[e : e + 1, :] for e in range(experts_dev)], axis=1)
        column = jnp.broadcast_to(row, (LANES, slots)).T
        lane = lax.broadcasted_iota(jnp.int32, (slots, tok_rows), 1)
        line = lax.broadcasted_iota(jnp.int32, (tok_rows, slots), 0)
        at = slice(side * slots, (side + 1) * slots)
        for q in range(first, LINE):
            for xr in range(PAIR):
                x_of = x if xr == 0 else 1 - x
                base = ((line_z(q) * PAIR + x_of) * dat_count + dat) * tok_rows
                start = ((q - first) * PAIR + xr) * tok_rows
                span = slice(start, start + tok_rows)
                pick[at, span] = (column == lane + base).astype(f32).astype(bf16)
                place[span, at] = (row == line + base).astype(f32).astype(bf16)

    one_hots(ids_ref, 0, pick_own, place_own, 0)

    pl.semaphore_wait(barrier, 5 + is_inner.astype(jnp.int32))

    def cross_copy(k):
        return copy_to(cross.at[k], blocks.at[k, spot, 1], x_sem, (k,), x_peer)

    ids_x = copy_to(ids_ref, ids_all.at[1], ids_sem, (0,), x_peer)
    ids_own = copy_to(ids_ref, ids_all.at[2], ids_sem, (1,), near)
    ids_fwd = copy_to(ids_all.at[1], ids_all.at[3], ids_sem, (2,), near)

    def near_copy(k, xr):
        return copy_to(blocks.at[k, 0, xr], blocks.at[k, 0, xr], near_sem, (k, xr), near)

    def far_copy(k, j, xr):
        return copy_to(blocks.at[k, 1 - j, xr], blocks.at[k, 2 + j, xr], far_sem, (k, j, xr), far_inner)

    def block_send(k, xr):
        send(far_copy(k, 1 - spot, xr))
        send(near_copy(k, xr), is_end)

    send(ids_x)
    send(ids_own, is_end)
    send(cross_copy(0))
    block_send(0, 0)
    for k in range(1, chunks):
        send(cross_copy(k))
        if k < chunks - 1:
            block_send(k, 0)
    ids_x.wait_recv()
    send(ids_fwd, is_end)
    one_hots(ids_all.at[1], 1, pick_own, place_own, 0)
    for k in range(chunks):
        cross_copy(k).wait_recv()
        block_send(k, 1)
        if k == 0:
            block_send(chunks - 1, 0)

    @pl.when(is_inner)
    def _():
        ids_own.wait_recv()
        ids_fwd.wait_recv()
        one_hots(ids_all.at[2], 0, pick_far, place_far, 1)
        one_hots(ids_all.at[3], 1, pick_far, place_far, 1)

    def pair(p):
        return slice(p * pair_e, (p + 1) * pair_e)

    def own_rows(k, rel, p, of_dat):
        feature = k * PAIR + (x if rel == 0 else 1 - x)
        at = pl.ds(pl.multiple_of(of_dat * cap_dev, cap_dev), cap_dev)
        return rows.at[feature, pair(p), at]

    def pick_copy(k, xr, p):
        return copy_to(
            pick_send.at[k, xr, pair(p)], pick_recv.at[k, xr, pair(p)], pick_sem, (k, xr, p), near
        )

    def swap_copy(k, p):
        at = pl.ds(pl.multiple_of(dat * cap_dev, cap_dev), cap_dev)
        return copy_to(
            swap_send.at[k, pair(p)], rows.at[k * PAIR + x, pair(p), at], swap_sem, (k, p), x_peer
        )

    def swap_arrival(k, p):
        return copy_to(
            swap_send.at[k, pair(p)], own_rows(k, 1, p, dat), swap_sem, (k, p), x_peer
        )

    def y_copy(k, rel, p, of_dat):
        ref = own_rows(k, rel, p, of_dat)
        return copy_to(ref, ref, y_sem, (k, rel, p), y_peer)

    def c_copy(k, rel, p, of_dat):
        ref = own_rows(k, rel, p, of_dat)
        return copy_to(ref, ref, c_sem, (k, rel, p), c_peer)

    def relay_copy(k, rel, p, of_dat):
        ref = own_rows(k, rel, p, of_dat)
        return copy_to(ref, ref, cr_sem, (k, rel, p), c_peer)

    dat_y = dat + PAIR - 2 * PAIR * y
    dat_c = dat + 1 - 2 * c
    dat_yc = dat_y + 1 - 2 * c

    def by_part(value):
        size = pair_e * cap_dev
        return [
            value[p * size : (p + 1) * size].reshape(pair_e, cap_dev, LANES) for p in range(PARTS)
        ]

    def stage_pick(k):
        @pl.when(is_inner)
        def _():
            for xr in range(PAIR):
                near_copy(k, xr).wait_recv()
                for j in range(2):
                    far_copy(k, j, xr).wait_recv()
            found = blocks[k].reshape(LINE * both, LANES)
            for xr in (1, 0):
                at = slice(xr * slots, (xr + 1) * slots)
                got = jnp.dot(pick_far[at, :], found[both:], preferred_element_type=f32)
                got = by_part(got.astype(bf16))
                for p in range(PARTS):
                    pick_send[k, xr, pair(p)] = got[p]
                    pick_copy(k, xr, p).start()
            got = jnp.dot(pick_own[slots:, :], found, preferred_element_type=f32)
            got = by_part(got.astype(bf16))
            for p in range(PARTS):
                swap_send[k, pair(p)] = got[p]
                swap_copy(k, p).start()
            got = jnp.dot(pick_own[:slots, :], found, preferred_element_type=f32)
            got = by_part(got.astype(bf16))
            for p in range(PARTS):
                own_rows(k, 0, p, dat)[...] = got[p]
                y_copy(k, 0, p, dat).start()
                c_copy(k, 0, p, dat).start()

        @pl.when(is_end)
        def _():
            found = blocks[k, 0].reshape(both, LANES)
            got = jnp.dot(pick_own[slots:, :both], found, preferred_element_type=f32)
            got = by_part(got)
            for p in range(PARTS):
                pick_copy(k, 1, p).wait_recv()
                swap_send[k, pair(p)] = (got[p] + pick_recv[k, 1, pair(p)].astype(f32)).astype(bf16)
                swap_copy(k, p).start()
            got = jnp.dot(pick_own[:slots, :both], found, preferred_element_type=f32)
            got = by_part(got)
            for p in range(PARTS):
                pick_copy(k, 0, p).wait_recv()
                own_rows(k, 0, p, dat)[...] = (
                    got[p] + pick_recv[k, 0, pair(p)].astype(f32)
                ).astype(bf16)
                y_copy(k, 0, p, dat).start()
                c_copy(k, 0, p, dat).start()

        for p in range(PARTS):
            for xr in range(PAIR):
                sent.append((pick_copy(k, xr, p), is_inner))
            sent.append((swap_copy(k, p), None))
            sent.append((y_copy(k, 0, p, dat), None))
            sent.append((c_copy(k, 0, p, dat), None))

    def stage_swap(k):
        for p in range(PARTS):
            swap_arrival(k, p).wait_recv()
            send(y_copy(k, 1, p, dat))
            send(c_copy(k, 1, p, dat))

    def stage_relay(k):
        for rel in range(PAIR):
            for p in range(PARTS):
                y_copy(k, rel, p, dat_y).wait_recv()
                send(relay_copy(k, rel, p, dat_y))

    def stage_first(k, p):
        for rel in range(PAIR):
            c_copy(k, rel, p, dat_c).wait_recv()
            relay_copy(k, rel, p, dat_yc).wait_recv()

        for e in range(p * pair_e, (p + 1) * pair_e):
            if k == 0:
                loads[e].wait()
            left = jnp.concatenate([rows[PAIR * k, e], rows[PAIR * k + 1, e]], axis=1)
            total = jnp.dot(left, inner_v[e, k * wide : (k + 1) * wide, :], preferred_element_type=f32)
            if k > 0:
                total += sums[e]
            if k + 1 < chunks:
                sums[e] = total
            else:
                hidden[e] = jnp.maximum(total, 0.0).astype(bf16)

    def core_copy(k, p):
        return copy_to(
            parts.at[k, :, 1 - c, pair(p)], core_recv.at[k, :, pair(p)], rc_sem, (k, p), c_peer
        )

    def back_y(k, p):
        return copy_to(y_send.at[k, pair(p)], y_recv.at[k, pair(p)], ry_sem, (k, p), y_peer)

    def back_x(k, p):
        return copy_to(give.at[k, pair(p)], slots_v.at[k, 1, pair(p)], rx_sem, (k, p), x_peer)

    def raw_copy(k, xr, p):
        return copy_to(
            slots_v.at[k, xr, pair(p)], raw.at[k, xr, pair(p)], raw_sem, (k, xr, p), near
        )

    def dest_copy(k, j, xr, peer):
        return copy_to(
            dest_send.at[k, j, xr], dest_recv.at[k, j, xr], dest_sem, (k, j, xr), peer
        )

    def last_copy(k):
        return copy_to(last_send.at[k], last_recv.at[k], last_sem, (k,), x_peer)

    def stage_second(k, p):
        for e in range(p * pair_e, (p + 1) * pair_e):
            if k == 0:
                loads[experts_dev + e].wait()
            part = jnp.dot(
                hidden[e], outer_v[e, :, k * wide : (k + 1) * wide], preferred_element_type=f32
            ).astype(bf16)
            for d in range(PAIR * PAIR):
                parts[k, d // PAIR, d % PAIR, e] = part[d * cap_dev : (d + 1) * cap_dev]
        send(core_copy(k, p))

    def stage_core(k, p):
        core_copy(k, p).wait_recv()
        theirs = parts[k, 1 - y, c, pair(p)].astype(f32) + core_recv[k, 1 - y, pair(p)].astype(f32)
        y_send[k, pair(p)] = theirs.astype(bf16)
        send(back_y(k, p))
        ours = parts[k, y, c, pair(p)].astype(f32) + core_recv[k, y, pair(p)].astype(f32)
        kept[k, pair(p)] = ours

    def gates():
        at = pl.ds(pl.multiple_of(dat * cap_dev, cap_dev), cap_dev)
        for e in range(experts_dev):
            score = jnp.zeros((cap_dev, LANES), f32)
            for b in range(PAIR * chunks):
                weight = router_ref[e : e + 1, b * LANES : (b + 1) * LANES].astype(f32)
                score += rows[b, e, at].astype(f32) * weight
            gate[e] = jax.nn.sigmoid(jnp.sum(score, axis=-1, keepdims=True))

    def stage_weigh(k, p):
        back_y(k, p).wait_recv()
        summed = kept[k, pair(p)] + y_recv[k, pair(p)].astype(f32)
        own, other = split(gate[pair(p)] * summed)
        give[k, pair(p)] = other.astype(bf16)
        send(back_x(k, p))
        slots_v[k, 0, pair(p)] = own.astype(bf16)
        send(raw_copy(k, 0, p), is_end)

    def stage_cross(k, p):
        back_x(k, p).wait_recv()
        send(raw_copy(k, 1, p), is_end)

    def dest_out(k, j, total, peer):
        for xr in (1, 0):
            dest_send[k, j, xr] = total[xr * tok_rows : (xr + 1) * tok_rows].astype(bf16)
            dest_copy(k, j, xr, peer).start()

    def stage_place(k):
        held = slots_v[k].reshape(PAIR * slots, LANES)

        @pl.when(is_inner)
        def _():
            dest_out(k, 0, jnp.dot(place_own[:both, :], held, preferred_element_type=f32), near)

        at = pl.ds(pl.multiple_of(spot * both, both), both)
        dense[k] = jnp.dot(place_own[at, :], held, preferred_element_type=f32)

    def stage_far(k):
        @pl.when(is_inner)
        def _():
            held = slots_v[k].reshape(PAIR * slots, LANES)
            mine = jnp.dot(place_own[2 * both :, :], held, preferred_element_type=f32)
            for xr in range(PAIR):
                for p in range(PARTS):
                    raw_copy(k, xr, p).wait_recv()
            ends = raw[k].reshape(PAIR * slots, LANES)
            mine += jnp.dot(place_far[both:, :], ends, preferred_element_type=f32)
            dest_out(k, 2, mine[both:], far_end)
            dest_out(k, 1, mine[:both], far_inner)
            dense[k] += jnp.dot(place_far[:both, :], ends, preferred_element_type=f32)

    def stage_total(k):
        for xr in range(PAIR):
            for j, peer in enumerate((near, far_inner, far_end)):
                sent.append((dest_copy(k, j, xr, peer), is_inner))

        def arrived(xr, j):
            dest_copy(k, j, xr, near).wait_recv()
            return dest_recv[k, j, xr].astype(f32)

        def finish(total, xr):
            if xr == 1:
                last_send[k] = total.astype(bf16)
                last_copy(k).start()
            else:
                last_own[k] = total

        @pl.when(is_end)
        def _():
            for xr in (1, 0):
                held = dense[k, xr * tok_rows : (xr + 1) * tok_rows]
                finish(held + arrived(xr, 0) + arrived(xr, 2), xr)

        @pl.when(is_inner)
        def _():
            for xr in (1, 0):
                held = dense[k, xr * tok_rows : (xr + 1) * tok_rows]
                finish(held + arrived(xr, 1), xr)

        sent.append((last_copy(k), None))

    def stage_last(k):
        last_copy(k).wait_recv()
        own, other = last_own[k], last_recv[k].astype(f32)
        cols = slice(k * wide, (k + 1) * wide)
        total = jnp.concatenate([jnp.where(x == 0, own, other), jnp.where(x == 0, other, own)], axis=1)
        out_ref[:, cols] = (tokens_ref[:, cols].astype(f32) + total).astype(bf16)

    for t in range(chunks + 3):
        if t < chunks:
            stage_pick(t)
        if 0 <= t - 1 < chunks:
            stage_swap(t - 1)
        if 0 <= t - 2 < chunks:
            stage_relay(t - 2)
        if 0 <= t - 3 < chunks:
            for p in range(PARTS):
                stage_first(t - 3, p)
                if t - 3 == chunks - 1:
                    stage_second(0, p)

    pieces = [(k, p) for k in range(chunks) for p in range(PARTS)]
    for i in range(PARTS, len(pieces)):
        stage_second(*pieces[i])
        stage_core(*pieces[i - PARTS])
    gates()
    for i in range(len(pieces) - PARTS, len(pieces)):
        stage_core(*pieces[i])

    for t in range(chunks + 4):
        if 0 <= t - 1 < chunks:
            stage_cross(t - 1, 0)
        if t < chunks:
            stage_weigh(t, 0)
        if 0 <= t - 2 < chunks:
            stage_far(t - 2)
        if 0 <= t - 1 < chunks:
            stage_cross(t - 1, 1)
            stage_place(t - 1)
        if t < chunks:
            stage_weigh(t, 1)
        if 0 <= t - 3 < chunks:
            stage_total(t - 3)
        if 0 <= t - 4 < chunks:
            stage_last(t - 4)

    for copy, cond in sent:
        if cond is None:
            copy.wait_send()
        else:
            pl.when(cond)(copy.wait_send)


def kernel_body(tokens, norm_gain, router_weight, inner_weight, outer_weight, slot_tokens, slot_ids):
    del slot_ids
    tok_rows, width = tokens.shape
    experts_dev, cap_dev = slot_tokens.shape
    units = inner_weight.shape[2]
    dat_count = lax.axis_size("dat")
    slots = experts_dev * cap_dev
    wide = PAIR * LANES
    chunks = width // wide
    both = PAIR * tok_rows
    bf16, f32 = jnp.bfloat16, jnp.float32
    vmem = pl.BlockSpec(memory_space=pltpu.VMEM)
    hbm = pl.BlockSpec(memory_space=pl.ANY)
    dma = pltpu.SemaphoreType.DMA

    def buffer(*shape, kind=bf16):
        return pltpu.VMEM(shape, kind)

    return pl.pallas_call(
        moe_kernel,
        out_shape=jax.ShapeDtypeStruct((tok_rows, width), bf16),
        in_specs=[vmem, vmem, vmem, vmem, hbm, hbm],
        out_specs=vmem,
        scratch_shapes=[
            buffer(experts_dev, width, units),
            buffer(experts_dev, units, width),
            buffer(LINE, experts_dev, cap_dev, kind=jnp.int32),
            buffer(PAIR * slots, LINE * both),
            buffer(LINE * both, PAIR * slots),
            buffer(PAIR * slots, (LINE - 1) * both),
            buffer((LINE - 1) * both, PAIR * slots),
            buffer(chunks, LINE, PAIR, tok_rows, LANES),
            buffer(chunks, tok_rows, LANES),
            buffer(chunks, PAIR, experts_dev, cap_dev, LANES),
            buffer(chunks, PAIR, experts_dev, cap_dev, LANES),
            buffer(chunks, experts_dev, cap_dev, LANES),
            buffer(PAIR * chunks, experts_dev, dat_count * cap_dev, LANES),
            buffer(experts_dev, dat_count * cap_dev, units, kind=f32),
            buffer(experts_dev, dat_count * cap_dev, units),
            buffer(experts_dev, cap_dev, 1, kind=f32),
            buffer(chunks, PAIR, PAIR, experts_dev, cap_dev, wide),
            buffer(chunks, PAIR, experts_dev, cap_dev, wide),
            buffer(chunks, experts_dev, cap_dev, wide),
            buffer(chunks, experts_dev, cap_dev, wide),
            buffer(chunks, experts_dev, cap_dev, wide, kind=f32),
            buffer(chunks, experts_dev, cap_dev, LANES),
            buffer(chunks, PAIR, experts_dev, cap_dev, LANES),
            buffer(chunks, PAIR, experts_dev, cap_dev, LANES),
            buffer(chunks, both, LANES, kind=f32),
            buffer(chunks, LINE - 1, PAIR, tok_rows, LANES),
            buffer(chunks, LINE - 1, PAIR, tok_rows, LANES),
            buffer(chunks, tok_rows, LANES),
            buffer(chunks, tok_rows, LANES),
            buffer(chunks, tok_rows, LANES, kind=f32),
            dma((2, experts_dev)),
            dma((2, 3)),
            dma((2, chunks)),
            dma((2, chunks, PAIR)),
            dma((2, chunks, 2, PAIR)),
            dma((2, chunks, PAIR, PARTS)),
            dma((2, chunks, PARTS)),
            dma((2, chunks, PAIR, PARTS)),
            dma((2, chunks, PAIR, PARTS)),
            dma((2, chunks, PAIR, PARTS)),
            dma((2, chunks, PARTS)),
            dma((2, chunks, PARTS)),
            dma((2, chunks, PARTS)),
            dma((2, chunks, PAIR, PARTS)),
            dma((2, chunks, LINE - 1, PAIR)),
            dma((2, chunks)),
        ],
        compiler_params=pltpu.CompilerParams(
            collective_id=0, has_side_effects=True, vmem_limit_bytes=60 * 1024 * 1024
        ),
    )(tokens, norm_gain.reshape(1, width), router_weight.T, slot_tokens, inner_weight, outer_weight)


def solution(mesh):
    fits = mesh.shape["dat"] == PAIR * PAIR and mesh.shape["exp"] == PAIR * LINE
    chosen = kernel_body if fits else body
    in_specs = (
        P(("exp", "dat"), None),
        P(),
        P(None, "exp"),
        P("exp", None, "dat"),
        P("exp", "dat", None),
        P("exp", "dat"),
        P(("exp", "dat"), None),
    )
    out_specs = P(("exp", "dat"), None)
    return jax.shard_map(chosen, mesh=mesh, in_specs=in_specs, out_specs=out_specs, check_vma=False)
```

time: 77.4 us -> 72 us (0.930)
  Pallas kernels: 75.6 us -> 70.2 us
    pallas_call x1, Pallas kernels: 75.6 us -> 70.2 us  [kernel_body(): pl.pallas_call(moe_kernel, out_shape=jax.ShapeDtypeStruct((tok_rows, widt...]
where the time goes in v1:
time: 72 us; the launch traced here: 71.9 us
  Pallas kernels  70.2 us (98%)
  local copies, waits for them, and re-layouts  1.67 us (2%)
    pallas_call x1, Pallas kernels, kernel_body(): pl.pallas_call(moe_kernel, out_shape=jax.ShapeDtypeStruct((tok_rows, widt...  70.2 us
    unnamed x1, local copies, waits for them, and re-layouts  1.67 us

profile of v1, /device:TPU:0, one launch (start us, length us, event | category | flops | bytes accessed | tf_op | source)
XLA Modules:
  0.0 71.9 jit_solution(4183771623998610993)
XLA Ops:
  0.0 70.2 %shard_map.64 = bf16[128,1024]{1,0:T(8,128)(2,1)} custom-call(bf16[128,1024]{1,0:T(8,128)(2,1)} %tokens_ref.1, f32[1,1024]{1,0:T(1,128)} %bitcast.3, bf16[4,1024]{1,0:T(4,128)(2,1)} %bitcast.2, s32[4,64]{1,0:T(4,128)} %ids_ref.1, bf16[4,1024,1024]{2,1,0:T(8,128)(2,1)} %inner_hbm.1, bf16[4,1024,1024]{2,1,0:T(8,128)(2,1)} %outer_hbm.1), custom_call_target="tpu_custom_call" | custom-call | tf_op jit(solution)/shard_map/pallas_call | solution.py:562
  70.2 1.7 %copy.8 = bf16[128,1024]{1,0:T(8,128)(2,1)} copy(bf16[128,1024]{1,0:T(8,128)(2,1)} %shard_map.64) | data formatting | bytes 524288

commit v2 on v1

--- a/solution.py
+++ b/solution.py
@@ -97,12 +97,12 @@
 
 
 def moe_kernel(
-    tokens_ref, gain_ref, router_ref, ids_ref, inner_hbm, outer_hbm, out_ref,
-    inner_v, outer_v, ids_all, pick_own, place_own, pick_far, place_far,
+    tokens_hbm, gain_hbm, router_hbm, ids_hbm, inner_hbm, outer_hbm, out_ref,
+    tokens_ref, gain_ref, router_ref, ids_ref, inner_v, outer_v, ids_all, pick_own, place_own, pick_far, place_far,
     blocks, cross, pick_send, pick_recv, swap_send, rows, sums, hidden, gate,
     parts, core_recv, y_send, y_recv, kept, give, slots_v, raw, dense, dest_send, dest_recv,
     last_send, last_recv, last_own,
-    w_sem, ids_sem, x_sem, near_sem, far_sem, pick_sem, swap_sem, y_sem, c_sem, cr_sem,
+    w_sem, out_sem, ids_sem, x_sem, near_sem, far_sem, pick_sem, swap_sem, y_sem, c_sem, cr_sem,
     rc_sem, ry_sem, rx_sem, raw_sem, dest_sem, last_sem,
 ):
     chunks = blocks.shape[0]
@@ -132,16 +132,15 @@
     x_peer = (exp + 1 - 2 * x, dat)
     y_peer = (exp, dat + PAIR - 2 * PAIR * y)
     c_peer = (exp, dat + 1 - 2 * c)
-    sent = []
-
-    def copy_to(src, dst, sems, where, peer):
+    diag = (line_z(1 - spot) * PAIR + 1 - x, dat)
+
+    def copy_to(src, dst, stage, sems, where, peer):
         return pltpu.make_async_remote_copy(
-            src_ref=src, dst_ref=dst, send_sem=sems.at[(0,) + where],
-            recv_sem=sems.at[(1,) + where], device_id=peer, device_id_type=MESH,
+            src_ref=src, dst_ref=dst, send_sem=out_sem.at[stage],
+            recv_sem=sems.at[where], device_id=peer, device_id_type=MESH,
         )
 
     def send(copy, cond=None):
-        sent.append((copy, cond))
         if cond is None:
             copy.start()
         else:
@@ -149,20 +148,30 @@
 
     loads = []
     for e in range(experts_dev):
-        loads.append(pltpu.make_async_copy(inner_hbm.at[e], inner_v.at[e], w_sem.at[0, e]))
+        loads.append(pltpu.make_async_copy(inner_hbm.at[e], inner_v.at[e], w_sem.at[0]))
     for e in range(experts_dev):
-        loads.append(pltpu.make_async_copy(outer_hbm.at[e], outer_v.at[e], w_sem.at[1, e]))
+        loads.append(pltpu.make_async_copy(outer_hbm.at[e], outer_v.at[e], w_sem.at[1]))
+    inner_load = pltpu.make_async_copy(inner_hbm, inner_v, w_sem.at[0])
+    outer_load = pltpu.make_async_copy(outer_hbm, outer_v, w_sem.at[1])
 
     barrier = pltpu.get_barrier_semaphore()
-    for peer in (near, far_inner, x_peer, y_peer, c_peer):
+    for peer in (near, diag, far_inner, x_peer, y_peer, c_peer):
         pl.semaphore_signal(barrier, inc=1, device_id=peer, device_id_type=MESH)
 
     @pl.when(is_inner)
     def _():
         pl.semaphore_signal(barrier, inc=1, device_id=far_end, device_id_type=MESH)
 
+    smalls = []
+    for i, (src, dst) in enumerate(
+        ((ids_hbm, ids_ref), (tokens_hbm, tokens_ref), (gain_hbm, gain_ref), (router_hbm, router_ref))
+    ):
+        smalls.append(pltpu.make_async_copy(src, dst, w_sem.at[2 + i]))
+        smalls[i].start()
     for load in loads:
         load.start()
+    smalls[1].wait()
+    smalls[2].wait()
 
     values = tokens_ref[...].astype(f32)
     scale = lax.rsqrt(jnp.mean(values * values, axis=-1, keepdims=True) + EPSILON)
@@ -192,48 +201,50 @@
                 pick[at, span] = (column == lane + base).astype(f32).astype(bf16)
                 place[span, at] = (row == line + base).astype(f32).astype(bf16)
 
+    smalls[0].wait()
     one_hots(ids_ref, 0, pick_own, place_own, 0)
 
-    pl.semaphore_wait(barrier, 5 + is_inner.astype(jnp.int32))
+    pl.semaphore_wait(barrier, 6 + is_inner.astype(jnp.int32))
 
     def cross_copy(k):
-        return copy_to(cross.at[k], blocks.at[k, spot, 1], x_sem, (k,), x_peer)
-
-    ids_x = copy_to(ids_ref, ids_all.at[1], ids_sem, (0,), x_peer)
-    ids_own = copy_to(ids_ref, ids_all.at[2], ids_sem, (1,), near)
-    ids_fwd = copy_to(ids_all.at[1], ids_all.at[3], ids_sem, (2,), near)
+        return copy_to(cross.at[k], blocks.at[k, spot, 1], 0, x_sem, (k,), x_peer)
+
+    ids_x = copy_to(ids_ref, ids_all.at[1], 1, ids_sem, (0,), x_peer)
+    ids_near = copy_to(ids_ref, ids_all.at[2], 2, ids_sem, (1,), near)
+    ids_diag = copy_to(ids_ref, ids_all.at[3], 2, ids_sem, (1,), diag)
+    ids_both = copy_to(ids_all.at[2:4], ids_all.at[2:4], 2, ids_sem, (1,), near)
 
     def near_copy(k, xr):
-        return copy_to(blocks.at[k, 0, xr], blocks.at[k, 0, xr], near_sem, (k, xr), near)
-
-    def far_copy(k, j, xr):
-        return copy_to(blocks.at[k, 1 - j, xr], blocks.at[k, 2 + j, xr], far_sem, (k, j, xr), far_inner)
+        ref = blocks.at[k, 0, xr]
+        return copy_to(ref, ref, 3, near_sem, (k,), near)
+
+    def far_copy(k, xr):
+        return copy_to(blocks.at[k, spot, xr], blocks.at[k, 3 - spot, xr], 4, far_sem, (k,), far_inner)
 
     def block_send(k, xr):
-        send(far_copy(k, 1 - spot, xr))
+        send(far_copy(k, xr))
         send(near_copy(k, xr), is_end)
 
-    send(ids_x)
-    send(ids_own, is_end)
     send(cross_copy(0))
     block_send(0, 0)
-    for k in range(1, chunks):
+    send(ids_x)
+    send(ids_near, is_end)
+    send(ids_diag, is_end)
+    send(cross_copy(1))
+    block_send(1, 0)
+    for k in range(2, chunks):
         send(cross_copy(k))
-        if k < chunks - 1:
-            block_send(k, 0)
-    ids_x.wait_recv()
-    send(ids_fwd, is_end)
-    one_hots(ids_all.at[1], 1, pick_own, place_own, 0)
     for k in range(chunks):
         cross_copy(k).wait_recv()
         block_send(k, 1)
-        if k == 0:
-            block_send(chunks - 1, 0)
+        if k + 2 < chunks:
+            block_send(k + 2, 0)
+    ids_x.wait_recv()
+    one_hots(ids_all.at[1], 1, pick_own, place_own, 0)
 
     @pl.when(is_inner)
     def _():
-        ids_own.wait_recv()
-        ids_fwd.wait_recv()
+        ids_both.wait_recv()
         one_hots(ids_all.at[2], 0, pick_far, place_far, 1)
         one_hots(ids_all.at[3], 1, pick_far, place_far, 1)
 
@@ -245,33 +256,33 @@
         at = pl.ds(pl.multiple_of(of_dat * cap_dev, cap_dev), cap_dev)
         return rows.at[feature, pair(p), at]
 
+    def dat_at(of_dat):
+        return pl.ds(pl.multiple_of(of_dat * cap_dev, cap_dev), cap_dev)
+
     def pick_copy(k, xr, p):
         return copy_to(
-            pick_send.at[k, xr, pair(p)], pick_recv.at[k, xr, pair(p)], pick_sem, (k, xr, p), near
+            pick_send.at[k, xr, pair(p)], pick_recv.at[k, xr, pair(p)], 5, pick_sem, (k, xr, p), near
         )
 
     def swap_copy(k, p):
-        at = pl.ds(pl.multiple_of(dat * cap_dev, cap_dev), cap_dev)
         return copy_to(
-            swap_send.at[k, pair(p)], rows.at[k * PAIR + x, pair(p), at], swap_sem, (k, p), x_peer
-        )
-
-    def swap_arrival(k, p):
-        return copy_to(
-            swap_send.at[k, pair(p)], own_rows(k, 1, p, dat), swap_sem, (k, p), x_peer
+            swap_send.at[k, pair(p)], own_rows(k, 0, p, dat), 6, swap_sem, (k, p), x_peer
         )
 
     def y_copy(k, rel, p, of_dat):
         ref = own_rows(k, rel, p, of_dat)
-        return copy_to(ref, ref, y_sem, (k, rel, p), y_peer)
+        return copy_to(ref, ref, 7, y_sem, (k, rel, p), y_peer)
 
     def c_copy(k, rel, p, of_dat):
         ref = own_rows(k, rel, p, of_dat)
-        return copy_to(ref, ref, c_sem, (k, rel, p), c_peer)
+        return copy_to(ref, ref, 8, c_sem, (k, p), c_peer)
 
     def relay_copy(k, rel, p, of_dat):
         ref = own_rows(k, rel, p, of_dat)
-        return copy_to(ref, ref, cr_sem, (k, rel, p), c_peer)
+        return copy_to(ref, ref, 9, cr_sem, (k, p), c_peer)
+
+    def both_rows(k, p, of_dat):
+        return rows.at[k * PAIR : (k + 1) * PAIR, pair(p), dat_at(of_dat)]
 
     dat_y = dat + PAIR - 2 * PAIR * y
     dat_c = dat + 1 - 2 * c
@@ -283,79 +294,75 @@
             value[p * size : (p + 1) * size].reshape(pair_e, cap_dev, LANES) for p in range(PARTS)
         ]
 
-    def stage_pick(k):
+    def sides(k):
+        return (1, 0) if k + 1 == chunks else (0, 1)
+
+    def stage_far_pick(k):
         @pl.when(is_inner)
         def _():
-            for xr in range(PAIR):
-                near_copy(k, xr).wait_recv()
-                for j in range(2):
-                    far_copy(k, j, xr).wait_recv()
+            near_all, far_all = blocks.at[k, 0], blocks.at[k, 2:4]
+            copy_to(near_all, near_all, 3, near_sem, (k,), near).wait_recv()
+            copy_to(far_all, far_all, 4, far_sem, (k,), far_inner).wait_recv()
             found = blocks[k].reshape(LINE * both, LANES)
-            for xr in (1, 0):
+            for xr in sides(k):
                 at = slice(xr * slots, (xr + 1) * slots)
                 got = jnp.dot(pick_far[at, :], found[both:], preferred_element_type=f32)
                 got = by_part(got.astype(bf16))
                 for p in range(PARTS):
                     pick_send[k, xr, pair(p)] = got[p]
                     pick_copy(k, xr, p).start()
-            got = jnp.dot(pick_own[slots:, :], found, preferred_element_type=f32)
-            got = by_part(got.astype(bf16))
-            for p in range(PARTS):
-                swap_send[k, pair(p)] = got[p]
-                swap_copy(k, p).start()
-            got = jnp.dot(pick_own[:slots, :], found, preferred_element_type=f32)
-            got = by_part(got.astype(bf16))
-            for p in range(PARTS):
-                own_rows(k, 0, p, dat)[...] = got[p]
-                y_copy(k, 0, p, dat).start()
-                c_copy(k, 0, p, dat).start()
+
+    def hand_on(k, xr, p, value):
+        if xr == 1:
+            swap_send[k, pair(p)] = value
+            swap_copy(k, p).start()
+        else:
+            own_rows(k, 0, p, dat)[...] = value
+            y_copy(k, 0, p, dat).start()
+            c_copy(k, 0, p, dat).start()
+
+    def stage_pick(k):
+        @pl.when(is_inner)
+        def _():
+            found = blocks[k].reshape(LINE * both, LANES)
+            for xr in (1, 0):
+                at = slice(xr * slots, (xr + 1) * slots)
+                got = jnp.dot(pick_own[at, :], found, preferred_element_type=f32)
+                got = by_part(got.astype(bf16))
+                for p in range(PARTS):
+                    hand_on(k, xr, p, got[p])
 
         @pl.when(is_end)
         def _():
             found = blocks[k, 0].reshape(both, LANES)
-            got = jnp.dot(pick_own[slots:, :both], found, preferred_element_type=f32)
-            got = by_part(got)
-            for p in range(PARTS):
-                pick_copy(k, 1, p).wait_recv()
-                swap_send[k, pair(p)] = (got[p] + pick_recv[k, 1, pair(p)].astype(f32)).astype(bf16)
-                swap_copy(k, p).start()
-            got = jnp.dot(pick_own[:slots, :both], found, preferred_element_type=f32)
-            got = by_part(got)
-            for p in range(PARTS):
-                pick_copy(k, 0, p).wait_recv()
-                own_rows(k, 0, p, dat)[...] = (
-                    got[p] + pick_recv[k, 0, pair(p)].astype(f32)
-                ).astype(bf16)
-                y_copy(k, 0, p, dat).start()
-                c_copy(k, 0, p, dat).start()
-
-        for p in range(PARTS):
-            for xr in range(PAIR):
-                sent.append((pick_copy(k, xr, p), is_inner))
-            sent.append((swap_copy(k, p), None))
-            sent.append((y_copy(k, 0, p, dat), None))
-            sent.append((c_copy(k, 0, p, dat), None))
+            for xr in sides(k):
+                at = slice(xr * slots, (xr + 1) * slots)
+                got = by_part(jnp.dot(pick_own[at, :both], found, preferred_element_type=f32))
+                for p in range(PARTS):
+                    pick_copy(k, xr, p).wait_recv()
+                    here = got[p] + pick_recv[k, xr, pair(p)].astype(f32)
+                    hand_on(k, xr, p, here.astype(bf16))
 
     def stage_swap(k):
         for p in range(PARTS):
-            swap_arrival(k, p).wait_recv()
+            ref = own_rows(k, 1, p, dat)
+            copy_to(ref, ref, 6, swap_sem, (k, p), x_peer).wait_recv()
             send(y_copy(k, 1, p, dat))
             send(c_copy(k, 1, p, dat))
 
-    def stage_relay(k):
-        for rel in range(PAIR):
-            for p in range(PARTS):
-                y_copy(k, rel, p, dat_y).wait_recv()
-                send(relay_copy(k, rel, p, dat_y))
+    def stage_relay(k, rel):
+        for p in range(PARTS):
+            y_copy(k, rel, p, dat_y).wait_recv()
+            send(relay_copy(k, rel, p, dat_y))
 
     def stage_first(k, p):
-        for rel in range(PAIR):
-            c_copy(k, rel, p, dat_c).wait_recv()
-            relay_copy(k, rel, p, dat_yc).wait_recv()
+        for sems, stage, of_dat in ((c_sem, 8, dat_c), (cr_sem, 9, dat_yc)):
+            ref = both_rows(k, p, of_dat)
+            copy_to(ref, ref, stage, sems, (k, p), c_peer).wait_recv()
+        if k == 0 and p == 0:
+            inner_load.wait()
 
         for e in range(p * pair_e, (p + 1) * pair_e):
-            if k == 0:
-                loads[e].wait()
             left = jnp.concatenate([rows[PAIR * k, e], rows[PAIR * k + 1, e]], axis=1)
             total = jnp.dot(left, inner_v[e, k * wide : (k + 1) * wide, :], preferred_element_type=f32)
             if k > 0:
@@ -367,32 +374,32 @@
 
     def core_copy(k, p):
         return copy_to(
-            parts.at[k, :, 1 - c, pair(p)], core_recv.at[k, :, pair(p)], rc_sem, (k, p), c_peer
+            parts.at[k, :, 1 - c, pair(p)], core_recv.at[k, :, pair(p)], 10, rc_sem, (k, p), c_peer
         )
 
     def back_y(k, p):
-        return copy_to(y_send.at[k, pair(p)], y_recv.at[k, pair(p)], ry_sem, (k, p), y_peer)
+        return copy_to(y_send.at[k, pair(p)], y_recv.at[k, pair(p)], 11, ry_sem, (k, p), y_peer)
 
     def back_x(k, p):
-        return copy_to(give.at[k, pair(p)], slots_v.at[k, 1, pair(p)], rx_sem, (k, p), x_peer)
+        return copy_to(give.at[k, pair(p)], slots_v.at[k, 1, pair(p)], 12, rx_sem, (k, p), x_peer)
 
     def raw_copy(k, xr, p):
         return copy_to(
-            slots_v.at[k, xr, pair(p)], raw.at[k, xr, pair(p)], raw_sem, (k, xr, p), near
+            slots_v.at[k, xr, pair(p)], raw.at[k, xr, pair(p)], 13, raw_sem, (k,), near
         )
 
     def dest_copy(k, j, xr, peer):
         return copy_to(
-            dest_send.at[k, j, xr], dest_recv.at[k, j, xr], dest_sem, (k, j, xr), peer
+            dest_send.at[k, j, xr], dest_recv.at[k, min(j, 1), xr], 14, dest_sem, (k, xr), peer
         )
 
     def last_copy(k):
-        return copy_to(last_send.at[k], last_recv.at[k], last_sem, (k,), x_peer)
+        return copy_to(last_send.at[k], last_recv.at[k], 15, last_sem, (k,), x_peer)
 
     def stage_second(k, p):
+        if k == 0 and p == 0:
+            outer_load.wait()
         for e in range(p * pair_e, (p + 1) * pair_e):
-            if k == 0:
-                loads[experts_dev + e].wait()
             part = jnp.dot(
                 hidden[e], outer_v[e, :, k * wide : (k + 1) * wide], preferred_element_type=f32
             ).astype(bf16)
@@ -409,6 +416,7 @@
         kept[k, pair(p)] = ours
 
     def gates():
+        smalls[3].wait()
         at = pl.ds(pl.multiple_of(dat * cap_dev, cap_dev), cap_dev)
         for e in range(experts_dev):
             score = jnp.zeros((cap_dev, LANES), f32)
@@ -450,9 +458,7 @@
         def _():
             held = slots_v[k].reshape(PAIR * slots, LANES)
             mine = jnp.dot(place_own[2 * both :, :], held, preferred_element_type=f32)
-            for xr in range(PAIR):
-                for p in range(PARTS):
-                    raw_copy(k, xr, p).wait_recv()
+            copy_to(raw.at[k], raw.at[k], 13, raw_sem, (k,), near).wait_recv()
             ends = raw[k].reshape(PAIR * slots, LANES)
             mine += jnp.dot(place_far[both:, :], ends, preferred_element_type=f32)
             dest_out(k, 2, mine[both:], far_end)
@@ -460,14 +466,6 @@
             dense[k] += jnp.dot(place_far[:both, :], ends, preferred_element_type=f32)
 
     def stage_total(k):
-        for xr in range(PAIR):
-            for j, peer in enumerate((near, far_inner, far_end)):
-                sent.append((dest_copy(k, j, xr, peer), is_inner))
-
-        def arrived(xr, j):
-            dest_copy(k, j, xr, near).wait_recv()
-            return dest_recv[k, j, xr].astype(f32)
-
         def finish(total, xr):
             if xr == 1:
                 last_send[k] = total.astype(bf16)
@@ -475,19 +473,21 @@
             else:
                 last_own[k] = total
 
+        def arrived(xr, ref):
+            copy_to(ref, ref, 14, dest_sem, (k, xr), near).wait_recv()
+            return dense[k, xr * tok_rows : (xr + 1) * tok_rows]
+
         @pl.when(is_end)
         def _():
             for xr in (1, 0):
-                held = dense[k, xr * tok_rows : (xr + 1) * tok_rows]
-                finish(held + arrived(xr, 0) + arrived(xr, 2), xr)
+                held = arrived(xr, dest_recv.at[k, :, xr])
+                finish(held + dest_recv[k, 0, xr].astype(f32) + dest_recv[k, 1, xr].astype(f32), xr)
 
         @pl.when(is_inner)
         def _():
             for xr in (1, 0):
-                held = dense[k, xr * tok_rows : (xr + 1) * tok_rows]
-                finish(held + arrived(xr, 1), xr)
-
-        sent.append((last_copy(k), None))
+                held = arrived(xr, dest_recv.at[k, 1, xr])
+                finish(held + dest_recv[k, 1, xr].astype(f32), xr)
 
     def stage_last(k):
         last_copy(k).wait_recv()
@@ -496,18 +496,26 @@
         total = jnp.concatenate([jnp.where(x == 0, own, other), jnp.where(x == 0, other, own)], axis=1)
         out_ref[:, cols] = (tokens_ref[:, cols].astype(f32) + total).astype(bf16)
 
-    for t in range(chunks + 3):
-        if t < chunks:
-            stage_pick(t)
-        if 0 <= t - 1 < chunks:
-            stage_swap(t - 1)
-        if 0 <= t - 2 < chunks:
-            stage_relay(t - 2)
-        if 0 <= t - 3 < chunks:
-            for p in range(PARTS):
-                stage_first(t - 3, p)
-                if t - 3 == chunks - 1:
-                    stage_second(0, p)
+    last = chunks - 1
+
+    def run_first(k):
+        for p in range(PARTS):
+            stage_first(k, p)
+            if k == last:
+                stage_second(0, p)
+
+    order = []
+    for k in range(chunks):
+        order += [
+            (2.8 * k - 2.65, stage_far_pick, (k,)),
+            (2.8 * k, stage_pick, (k,)),
+            (2.8 * k + 3.1, stage_swap, (k,)),
+            (2.8 * k + 3.9, stage_relay, (k, 0)),
+            (2.8 * k + 7.0, stage_relay, (k, 1)),
+            (2.8 * k + 8.9, run_first, (k,)),
+        ]
+    for _, stage, where in sorted(order, key=lambda step: step[0]):
+        stage(*where)
 
     pieces = [(k, p) for k in range(chunks) for p in range(PARTS)]
     for i in range(PARTS, len(pieces)):
@@ -517,28 +525,46 @@
     for i in range(len(pieces) - PARTS, len(pieces)):
         stage_core(*pieces[i])
 
-    for t in range(chunks + 4):
-        if 0 <= t - 1 < chunks:
-            stage_cross(t - 1, 0)
+    for i in range(len(pieces) + 2):
+        if i < len(pieces):
+            stage_weigh(*pieces[i])
+        if i == len(pieces):
+            stage_far(0)
+        if i >= 2:
+            stage_cross(*pieces[i - 2])
+            if i % 2 == 1:
+                stage_place(i // 2 - 1)
+    for t in range(1, chunks + 3):
         if t < chunks:
-            stage_weigh(t, 0)
-        if 0 <= t - 2 < chunks:
-            stage_far(t - 2)
-        if 0 <= t - 1 < chunks:
-            stage_cross(t - 1, 1)
-            stage_place(t - 1)
-        if t < chunks:
-            stage_weigh(t, 1)
-        if 0 <= t - 3 < chunks:
-            stage_total(t - 3)
-        if 0 <= t - 4 < chunks:
-            stage_last(t - 4)
-
-    for copy, cond in sent:
+            stage_far(t)
+        if t >= 3:
+            stage_last(t - 3)
+        if 1 <= t <= chunks:
+            stage_total(t - 1)
+
+    def sent(ref, stage, cond=None):
+        done = copy_to(ref, ref, stage, ids_sem, (0,), x_peer)
         if cond is None:
-            copy.wait_send()
+            done.wait_send()
         else:
-            pl.when(cond)(copy.wait_send)
+            pl.when(cond)(done.wait_send)
+
+    own_all = rows.at[:, :, dat_at(dat)]
+    sent(cross, 0)
+    sent(ids_ref, 1)
+    sent(ids_all.at[2:4], 2, is_end)
+    sent(blocks.at[0], 3, is_end)
+    sent(blocks.at[0], 4)
+    sent(pick_send, 5, is_inner)
+    sent(swap_send, 6)
+    for stage in (7, 8, 9):
+        sent(own_all, stage)
+    sent(parts.at[:, :, 1 - c], 10)
+    sent(y_send, 11)
+    sent(give, 12)
+    sent(slots_v, 13, is_end)
+    sent(dest_send, 14, is_inner)
+    sent(last_send, 15)
 
 
 def kernel_body(tokens, norm_gain, router_weight, inner_weight, outer_weight, slot_tokens, slot_ids):
@@ -553,7 +579,7 @@
     both = PAIR * tok_rows
     bf16, f32 = jnp.bfloat16, jnp.float32
     vmem = pl.BlockSpec(memory_space=pltpu.VMEM)
-    hbm = pl.BlockSpec(memory_space=pl.ANY)
+    hbm = pl.BlockSpec(memory_space=pltpu.HBM)
     dma = pltpu.SemaphoreType.DMA
 
     def buffer(*shape, kind=bf16):
@@ -562,9 +588,13 @@
     return pl.pallas_call(
         moe_kernel,
         out_shape=jax.ShapeDtypeStruct((tok_rows, width), bf16),
-        in_specs=[vmem, vmem, vmem, vmem, hbm, hbm],
+        in_specs=[hbm] * 6,
         out_specs=vmem,
         scratch_shapes=[
+            buffer(tok_rows, width),
+            buffer(1, width, kind=f32),
+            buffer(experts_dev, width),
+            buffer(experts_dev, cap_dev, kind=jnp.int32),
             buffer(experts_dev, width, units),
             buffer(experts_dev, units, width),
             buffer(LINE, experts_dev, cap_dev, kind=jnp.int32),
@@ -591,31 +621,39 @@
             buffer(chunks, PAIR, experts_dev, cap_dev, LANES),
             buffer(chunks, both, LANES, kind=f32),
             buffer(chunks, LINE - 1, PAIR, tok_rows, LANES),
-            buffer(chunks, LINE - 1, PAIR, tok_rows, LANES),
+            buffer(chunks, 2, PAIR, tok_rows, LANES),
             buffer(chunks, tok_rows, LANES),
             buffer(chunks, tok_rows, LANES),
             buffer(chunks, tok_rows, LANES, kind=f32),
-            dma((2, experts_dev)),
-            dma((2, 3)),
-            dma((2, chunks)),
-            dma((2, chunks, PAIR)),
-            dma((2, chunks, 2, PAIR)),
-            dma((2, chunks, PAIR, PARTS)),
-            dma((2, chunks, PARTS)),
-            dma((2, chunks, PAIR, PARTS)),
-            dma((2, chunks, PAIR, PARTS)),
-            dma((2, chunks, PAIR, PARTS)),
-            dma((2, chunks, PARTS)),
-            dma((2, chunks, PARTS)),
-            dma((2, chunks, PARTS)),
-            dma((2, chunks, PAIR, PARTS)),
-            dma((2, chunks, LINE - 1, PAIR)),
-            dma((2, chunks)),
+            dma((6,)),
+            dma((16,)),
+            dma((2,)),
+            dma((chunks,)),
+            dma((chunks,)),
+            dma((chunks,)),
+            dma((chunks, PAIR, PARTS)),
+            dma((chunks, PARTS)),
+            dma((chunks, PAIR, PARTS)),
+            dma((chunks, PARTS)),
+            dma((chunks, PARTS)),
+            dma((chunks, PARTS)),
+            dma((chunks, PARTS)),
+            dma((chunks, PARTS)),
+            dma((chunks,)),
+            dma((chunks, PAIR)),
+            dma((chunks,)),
         ],
         compiler_params=pltpu.CompilerParams(
-            collective_id=0, has_side_effects=True, vmem_limit_bytes=60 * 1024 * 1024
+            collective_id=0, has_side_effects=True, vmem_limit_bytes=48 * 1024 * 1024
         ),
-    )(tokens, norm_gain.reshape(1, width), router_weight.T, slot_tokens, inner_weight, outer_weight)
+    )(
+        *(
+            pltpu.with_memory_space_constraint(array, pltpu.HBM)
+            for array in (tokens, norm_gain.reshape(1, width), router_weight.T, slot_tokens)
+        ),
+        inner_weight,
+        outer_weight,
+    )
 
 
 def solution(mesh):

time: 72 us -> 63.7 us (0.88)
  Pallas kernels: 70.2 us -> 62.9 us
  local copies, waits for them, and re-layouts: 1.67 us -> 0.71 us
    pallas_call x1, Pallas kernels: 70.2 us -> 62.9 us  [kernel_body(): pl.pallas_call(moe_kernel, out_shape=jax.ShapeDtypeStruct((tok_rows, widt...]
    unnamed x1, local copies, waits for them, and re-layouts: 1.67 us -> 0.71 us
where the time goes in v2:
time: 63.7 us; the launch traced here: 63.6 us
  Pallas kernels  62.9 us (99%)
  local copies, waits for them, and re-layouts  0.71 us (1%)
    pallas_call x1, Pallas kernels, kernel_body(): pl.pallas_call(moe_kernel, out_shape=jax.ShapeDtypeStruct((tok_rows, widt...  62.9 us

profile of v2, /device:TPU:0, one launch (start us, length us, event | category | flops | bytes accessed | tf_op | source)
XLA Modules:
  0.0 63.6 jit_solution(692910750883847179)
XLA Ops:
  0.0 62.9 %shard_map.64 = bf16[128,1024]{1,0:T(8,128)(2,1)S(1)} custom-call(bf16[128,1024]{1,0:T(8,128)(2,1)} %tokens_hbm.1, f32[1,1024]{1,0:T(1,128)} %bitcast.3, bf16[4,1024]{1,0:T(4,128)(2,1)} %bitcast.2, s32[4,64]{1,0:T(4,128)} %ids_hbm.1, bf16[4,1024,1024]{2,1,0:T(8,128)(2,1)} %inner_hbm.1, bf16[4,1024,1024]{2,1,0:T(8,128)(2,1)} %outer_hbm.1), custom_call_target="tpu_custom_call" | custom-call | tf_op jit(solution)/shard_map/pallas_call | solution.py:588
  62.9 0.7 %copy.8 = bf16[128,1024]{1,0:T(8,128)(2,1)} copy(bf16[128,1024]{1,0:T(8,128)(2,1)S(1)} %shard_map.64) | data formatting | bytes 524288

commit v3 on v2

--- a/solution.py
+++ b/solution.py
@@ -94,6 +94,7 @@
 LINE = 4
 LANES = 128
 PARTS = 2
+CROSS_IN = (-2.8, -5.5, -5.0, -1.9)
 
 
 def moe_kernel(
@@ -132,7 +133,11 @@
     x_peer = (exp + 1 - 2 * x, dat)
     y_peer = (exp, dat + PAIR - 2 * PAIR * y)
     c_peer = (exp, dat + 1 - 2 * c)
-    diag = (line_z(1 - spot) * PAIR + 1 - x, dat)
+    near_diag = (line_z(1 - spot) * PAIR + 1 - x, dat)
+    far_diag = (line_z(2) * PAIR + 1 - x, dat)
+    far_end_diag = (line_z(3) * PAIR + 1 - x, dat)
+    xy_diag = (exp + 1 - 2 * x, dat + PAIR - 2 * PAIR * y)
+    last = chunks - 1
 
     def copy_to(src, dst, stage, sems, where, peer):
         return pltpu.make_async_remote_copy(
@@ -155,12 +160,13 @@
     outer_load = pltpu.make_async_copy(outer_hbm, outer_v, w_sem.at[1])
 
     barrier = pltpu.get_barrier_semaphore()
-    for peer in (near, diag, far_inner, x_peer, y_peer, c_peer):
+    for peer in (near, near_diag, far_inner, far_diag, x_peer, y_peer, xy_diag, c_peer):
         pl.semaphore_signal(barrier, inc=1, device_id=peer, device_id_type=MESH)
 
     @pl.when(is_inner)
     def _():
-        pl.semaphore_signal(barrier, inc=1, device_id=far_end, device_id_type=MESH)
+        for peer in (far_end, far_end_diag):
+            pl.semaphore_signal(barrier, inc=1, device_id=peer, device_id_type=MESH)
 
     smalls = []
     for i, (src, dst) in enumerate(
@@ -204,14 +210,14 @@
     smalls[0].wait()
     one_hots(ids_ref, 0, pick_own, place_own, 0)
 
-    pl.semaphore_wait(barrier, 6 + is_inner.astype(jnp.int32))
+    pl.semaphore_wait(barrier, 8 + 2 * is_inner.astype(jnp.int32))
 
     def cross_copy(k):
         return copy_to(cross.at[k], blocks.at[k, spot, 1], 0, x_sem, (k,), x_peer)
 
     ids_x = copy_to(ids_ref, ids_all.at[1], 1, ids_sem, (0,), x_peer)
     ids_near = copy_to(ids_ref, ids_all.at[2], 2, ids_sem, (1,), near)
-    ids_diag = copy_to(ids_ref, ids_all.at[3], 2, ids_sem, (1,), diag)
+    ids_diag = copy_to(ids_ref, ids_all.at[3], 2, ids_sem, (1,), near_diag)
     ids_both = copy_to(ids_all.at[2:4], ids_all.at[2:4], 2, ids_sem, (1,), near)
 
     def near_copy(k, xr):
@@ -225,28 +231,39 @@
         send(far_copy(k, xr))
         send(near_copy(k, xr), is_end)
 
-    send(cross_copy(0))
-    block_send(0, 0)
+    def diag_send(k):
+        send(copy_to(cross.at[k], blocks.at[k, 3 - spot, 1], 4, far_sem, (k,), far_diag))
+        send(copy_to(cross.at[k], blocks.at[k, 0, 1], 3, near_sem, (k,), near_diag), is_end)
+
     send(ids_x)
     send(ids_near, is_end)
     send(ids_diag, is_end)
+    diag_send(0)
+    block_send(0, 0)
     send(cross_copy(1))
     block_send(1, 0)
+    send(cross_copy(0))
+    block_send(2, 0)
     for k in range(2, chunks):
         send(cross_copy(k))
-    for k in range(chunks):
+
+    def stage_cross_in(k):
         cross_copy(k).wait_recv()
-        block_send(k, 1)
-        if k + 2 < chunks:
-            block_send(k + 2, 0)
-    ids_x.wait_recv()
-    one_hots(ids_all.at[1], 1, pick_own, place_own, 0)
-
-    @pl.when(is_inner)
-    def _():
-        ids_both.wait_recv()
-        one_hots(ids_all.at[2], 0, pick_far, place_far, 1)
-        one_hots(ids_all.at[3], 1, pick_far, place_far, 1)
+        if k > 0:
+            block_send(k, 1)
+        if k == 1:
+            for j in range(3, chunks):
+                block_send(j, 0)
+
+    def stage_ids():
+        ids_x.wait_recv()
+        one_hots(ids_all.at[1], 1, pick_own, place_own, 0)
+
+        @pl.when(is_inner)
+        def _():
+            ids_both.wait_recv()
+            one_hots(ids_all.at[2], 0, pick_far, place_far, 1)
+            one_hots(ids_all.at[3], 1, pick_far, place_far, 1)
 
     def pair(p):
         return slice(p * pair_e, (p + 1) * pair_e)
@@ -267,6 +284,11 @@
     def swap_copy(k, p):
         return copy_to(
             swap_send.at[k, pair(p)], own_rows(k, 0, p, dat), 6, swap_sem, (k, p), x_peer
+        )
+
+    def far_swap(k, p):
+        return copy_to(
+            swap_send.at[k, pair(p)], own_rows(k, 0, p, dat), 7, y_sem, (k, 1, p), xy_diag
         )
 
     def y_copy(k, rel, p, of_dat):
@@ -316,6 +338,7 @@
         if xr == 1:
             swap_send[k, pair(p)] = value
             swap_copy(k, p).start()
+            far_swap(k, p).start()
         else:
             own_rows(k, 0, p, dat)[...] = value
             y_copy(k, 0, p, dat).start()
@@ -347,7 +370,6 @@
         for p in range(PARTS):
             ref = own_rows(k, 1, p, dat)
             copy_to(ref, ref, 6, swap_sem, (k, p), x_peer).wait_recv()
-            send(y_copy(k, 1, p, dat))
             send(c_copy(k, 1, p, dat))
 
     def stage_relay(k, rel):
@@ -430,28 +452,39 @@
         summed = kept[k, pair(p)] + y_recv[k, pair(p)].astype(f32)
         own, other = split(gate[pair(p)] * summed)
         give[k, pair(p)] = other.astype(bf16)
+        ref = raw.at[k, 1, pair(p)]
+        send(copy_to(give.at[k, pair(p)], ref, 13, raw_sem, (k,), near_diag), is_end)
         send(back_x(k, p))
         slots_v[k, 0, pair(p)] = own.astype(bf16)
         send(raw_copy(k, 0, p), is_end)
 
     def stage_cross(k, p):
         back_x(k, p).wait_recv()
-        send(raw_copy(k, 1, p), is_end)
-
-    def dest_out(k, j, total, peer):
+
+    def dest_out(k, j, total, peer, peer_diag):
         for xr in (1, 0):
             dest_send[k, j, xr] = total[xr * tok_rows : (xr + 1) * tok_rows].astype(bf16)
-            dest_copy(k, j, xr, peer).start()
+            dest_copy(k, j, xr, peer_diag if k == last and xr == 1 else peer).start()
+
+    def last_out(k, total):
+        last_send[k] = total.astype(bf16)
+        last_copy(k).start()
 
     def stage_place(k):
         held = slots_v[k].reshape(PAIR * slots, LANES)
 
         @pl.when(is_inner)
         def _():
-            dest_out(k, 0, jnp.dot(place_own[:both, :], held, preferred_element_type=f32), near)
+            dest_out(k, 0, jnp.dot(place_own[:both, :], held, preferred_element_type=f32), near, near_diag)
 
         at = pl.ds(pl.multiple_of(spot * both, both), both)
-        dense[k] = jnp.dot(place_own[at, :], held, preferred_element_type=f32)
+        total = jnp.dot(place_own[at, :], held, preferred_element_type=f32)
+        dense[k] = total
+        if k == last:
+
+            @pl.when(is_end)
+            def _():
+                last_out(k, total[tok_rows:])
 
     def stage_far(k):
         @pl.when(is_inner)
@@ -461,42 +494,61 @@
             copy_to(raw.at[k], raw.at[k], 13, raw_sem, (k,), near).wait_recv()
             ends = raw[k].reshape(PAIR * slots, LANES)
             mine += jnp.dot(place_far[both:, :], ends, preferred_element_type=f32)
-            dest_out(k, 2, mine[both:], far_end)
-            dest_out(k, 1, mine[:both], far_inner)
-            dense[k] += jnp.dot(place_far[:both, :], ends, preferred_element_type=f32)
+            dest_out(k, 2, mine[both:], far_end, far_end_diag)
+            dest_out(k, 1, mine[:both], far_inner, far_diag)
+            total = dense[k] + jnp.dot(place_far[:both, :], ends, preferred_element_type=f32)
+            dense[k] = total
+            if k == last:
+                last_out(k, total[tok_rows:])
+
+    def arrived(k, xr, ref):
+        copy_to(ref, ref, 14, dest_sem, (k, xr), near).wait_recv()
 
     def stage_total(k):
         def finish(total, xr):
             if xr == 1:
-                last_send[k] = total.astype(bf16)
-                last_copy(k).start()
+                last_out(k, total)
             else:
                 last_own[k] = total
 
-        def arrived(xr, ref):
-            copy_to(ref, ref, 14, dest_sem, (k, xr), near).wait_recv()
-            return dense[k, xr * tok_rows : (xr + 1) * tok_rows]
+        where = (0,) if k == last else (1, 0)
 
         @pl.when(is_end)
         def _():
-            for xr in (1, 0):
-                held = arrived(xr, dest_recv.at[k, :, xr])
+            for xr in where:
+                arrived(k, xr, dest_recv.at[k, :, xr])
+                held = dense[k, xr * tok_rows : (xr + 1) * tok_rows]
                 finish(held + dest_recv[k, 0, xr].astype(f32) + dest_recv[k, 1, xr].astype(f32), xr)
 
         @pl.when(is_inner)
         def _():
-            for xr in (1, 0):
-                held = arrived(xr, dest_recv.at[k, 1, xr])
+            for xr in where:
+                arrived(k, xr, dest_recv.at[k, 1, xr])
+                held = dense[k, xr * tok_rows : (xr + 1) * tok_rows]
                 finish(held + dest_recv[k, 1, xr].astype(f32), xr)
 
     def stage_last(k):
+        def finish(own, other):
+            cols = slice(k * wide, (k + 1) * wide)
+            left, right = jnp.where(x == 0, own, other), jnp.where(x == 0, other, own)
+            total = jnp.concatenate([left, right], axis=1)
+            out_ref[:, cols] = (tokens_ref[:, cols].astype(f32) + total).astype(bf16)
+
         last_copy(k).wait_recv()
         own, other = last_own[k], last_recv[k].astype(f32)
-        cols = slice(k * wide, (k + 1) * wide)
-        total = jnp.concatenate([jnp.where(x == 0, own, other), jnp.where(x == 0, other, own)], axis=1)
-        out_ref[:, cols] = (tokens_ref[:, cols].astype(f32) + total).astype(bf16)
-
-    last = chunks - 1
+        if k < last:
+            finish(own, other)
+            return
+
+        @pl.when(is_end)
+        def _():
+            arrived(k, 1, dest_recv.at[k, :, 1])
+            finish(own, other + dest_recv[k, 0, 1].astype(f32) + dest_recv[k, 1, 1].astype(f32))
+
+        @pl.when(is_inner)
+        def _():
+            arrived(k, 1, dest_recv.at[k, 1, 1])
+            finish(own, other + dest_recv[k, 1, 1].astype(f32))
 
     def run_first(k):
         for p in range(PARTS):
@@ -504,9 +556,10 @@
             if k == last:
                 stage_second(0, p)
 
-    order = []
+    order = [(-6.0, stage_ids, ())]
     for k in range(chunks):
         order += [
+            (CROSS_IN[k], stage_cross_in, (k,)),
             (2.8 * k - 2.65, stage_far_pick, (k,)),
             (2.8 * k, stage_pick, (k,)),
             (2.8 * k + 3.1, stage_swap, (k,)),
@@ -525,22 +578,20 @@
     for i in range(len(pieces) - PARTS, len(pieces)):
         stage_core(*pieces[i])
 
-    for i in range(len(pieces) + 2):
-        if i < len(pieces):
-            stage_weigh(*pieces[i])
-        if i == len(pieces):
-            stage_far(0)
-        if i >= 2:
-            stage_cross(*pieces[i - 2])
-            if i % 2 == 1:
-                stage_place(i // 2 - 1)
-    for t in range(1, chunks + 3):
-        if t < chunks:
-            stage_far(t)
-        if t >= 3:
-            stage_last(t - 3)
-        if 1 <= t <= chunks:
-            stage_total(t - 1)
+    order = []
+    for k in range(chunks):
+        order += [
+            (2 * k + 0.0, stage_weigh, (k, 0)),
+            (2 * k + 1.0, stage_weigh, (k, 1)),
+            (2 * k + 2.1, stage_cross, (k, 0)),
+            (2 * k + 3.1, stage_cross, (k, 1)),
+            (2 * k + 3.2, stage_place, (k,)),
+            (2 * k + 7.05, stage_far, (k,)),
+            (2 * k + 11.4, stage_total, (k,)),
+            (2 * k + 15.6, stage_last, (k,)),
+        ]
+    for _, stage, where in sorted(order, key=lambda step: step[0]):
+        stage(*where)
 
     def sent(ref, stage, cond=None):
         done = copy_to(ref, ref, stage, ids_sem, (0,), x_peer)

time: 63.7 us -> 60.2 us (0.945)
  Pallas kernels: 62.9 us -> 59.4 us
    pallas_call x1, Pallas kernels: 62.9 us -> 59.4 us  [kernel_body(): pl.pallas_call(moe_kernel, out_shape=jax.ShapeDtypeStruct((tok_rows, widt...]
where the time goes in v3:
time: 60.2 us; the launch traced here: 60.1 us
  Pallas kernels  59.4 us (99%)
  local copies, waits for them, and re-layouts  0.71 us (1%)
    pallas_call x1, Pallas kernels, kernel_body(): pl.pallas_call(moe_kernel, out_shape=jax.ShapeDtypeStruct((tok_rows, widt...  59.4 us

profile of v3, /device:TPU:0, one launch (start us, length us, event | category | flops | bytes accessed | tf_op | source)
XLA Modules:
  0.0 60.1 jit_solution(2833215332553194791)
XLA Ops:
  0.0 59.4 %shard_map.64 = bf16[128,1024]{1,0:T(8,128)(2,1)S(1)} custom-call(bf16[128,1024]{1,0:T(8,128)(2,1)} %tokens_hbm.1, f32[1,1024]{1,0:T(1,128)} %bitcast.3, bf16[4,1024]{1,0:T(4,128)(2,1)} %bitcast.2, s32[4,64]{1,0:T(4,128)} %ids_hbm.1, bf16[4,1024,1024]{2,1,0:T(8,128)(2,1)} %inner_hbm.1, bf16[4,1024,1024]{2,1,0:T(8,128)(2,1)} %outer_hbm.1), custom_call_target="tpu_custom_call" | custom-call | tf_op jit(solution)/shard_map/pallas_call | solution.py:639
  59.4 0.7 %copy.8 = bf16[128,1024]{1,0:T(8,128)(2,1)} copy(bf16[128,1024]{1,0:T(8,128)(2,1)S(1)} %shard_map.64) | data formatting | bytes 524288

commit v4 on v3

--- a/solution.py
+++ b/solution.py
@@ -94,7 +94,9 @@
 LINE = 4
 LANES = 128
 PARTS = 2
-CROSS_IN = (-2.8, -5.5, -5.0, -1.9)
+FIRST_AT = (9.6, 11.3, 14.5, 16.8)
+RELAY_AT = (5.65, 8.45, 11.25, 12.4)
+CROSS_IN = (-5.5, -5.4, -2.6, -1.9)
 
 
 def moe_kernel(
@@ -238,11 +240,11 @@
     send(ids_x)
     send(ids_near, is_end)
     send(ids_diag, is_end)
+    send(cross_copy(0))
     diag_send(0)
     block_send(0, 0)
     send(cross_copy(1))
     block_send(1, 0)
-    send(cross_copy(0))
     block_send(2, 0)
     for k in range(2, chunks):
         send(cross_copy(k))
@@ -493,9 +495,10 @@
             mine = jnp.dot(place_own[2 * both :, :], held, preferred_element_type=f32)
             copy_to(raw.at[k], raw.at[k], 13, raw_sem, (k,), near).wait_recv()
             ends = raw[k].reshape(PAIR * slots, LANES)
-            mine += jnp.dot(place_far[both:, :], ends, preferred_element_type=f32)
-            dest_out(k, 2, mine[both:], far_end, far_end_diag)
-            dest_out(k, 1, mine[:both], far_inner, far_diag)
+            theirs = jnp.dot(place_far[2 * both :, :], ends, preferred_element_type=f32)
+            dest_out(k, 2, mine[both:] + theirs, far_end, far_end_diag)
+            theirs = jnp.dot(place_far[both : 2 * both, :], ends, preferred_element_type=f32)
+            dest_out(k, 1, mine[:both] + theirs, far_inner, far_diag)
             total = dense[k] + jnp.dot(place_far[:both, :], ends, preferred_element_type=f32)
             dense[k] = total
             if k == last:
@@ -564,8 +567,8 @@
             (2.8 * k, stage_pick, (k,)),
             (2.8 * k + 3.1, stage_swap, (k,)),
             (2.8 * k + 3.9, stage_relay, (k, 0)),
-            (2.8 * k + 7.0, stage_relay, (k, 1)),
-            (2.8 * k + 8.9, run_first, (k,)),
+            (RELAY_AT[k], stage_relay, (k, 1)),
+            (FIRST_AT[k], run_first, (k,)),
         ]
     for _, stage, where in sorted(order, key=lambda step: step[0]):
         stage(*where)
@@ -586,7 +589,7 @@
             (2 * k + 2.1, stage_cross, (k, 0)),
             (2 * k + 3.1, stage_cross, (k, 1)),
             (2 * k + 3.2, stage_place, (k,)),
-            (2 * k + 7.05, stage_far, (k,)),
+            (2 * k + 6.05, stage_far, (k,)),
             (2 * k + 11.4, stage_total, (k,)),
             (2 * k + 15.6, stage_last, (k,)),
         ]

time: 60.2 us -> 56.8 us (0.944)
  Pallas kernels: 59.4 us -> 56 us
    pallas_call x1, Pallas kernels: 59.4 us -> 56 us  [kernel_body(): pl.pallas_call(moe_kernel, out_shape=jax.ShapeDtypeStruct((tok_rows, widt...]
where the time goes in v4:
time: 56.8 us; the launch traced here: 56.7 us
  Pallas kernels  56 us (99%)
  local copies, waits for them, and re-layouts  0.71 us (1%)
    pallas_call x1, Pallas kernels, kernel_body(): pl.pallas_call(moe_kernel, out_shape=jax.ShapeDtypeStruct((tok_rows, widt...  56 us

profile of v4, /device:TPU:0, one launch (start us, length us, event | category | flops | bytes accessed | tf_op | source)
XLA Modules:
  0.0 56.7 jit_solution(880940495270758201)
XLA Ops:
  0.0 56.0 %shard_map.64 = bf16[128,1024]{1,0:T(8,128)(2,1)S(1)} custom-call(bf16[128,1024]{1,0:T(8,128)(2,1)} %tokens_hbm.1, f32[1,1024]{1,0:T(1,128)} %bitcast.3, bf16[4,1024]{1,0:T(4,128)(2,1)} %bitcast.2, s32[4,64]{1,0:T(4,128)} %ids_hbm.1, bf16[4,1024,1024]{2,1,0:T(8,128)(2,1)} %inner_hbm.1, bf16[4,1024,1024]{2,1,0:T(8,128)(2,1)} %outer_hbm.1), custom_call_target="tpu_custom_call" | custom-call | tf_op jit(solution)/shard_map/pallas_call | solution.py:642
  56.0 0.7 %copy.8 = bf16[128,1024]{1,0:T(8,128)(2,1)} copy(bf16[128,1024]{1,0:T(8,128)(2,1)S(1)} %shard_map.64) | data formatting | bytes 524288

commit v5 on v4

--- a/solution.py
+++ b/solution.py
@@ -94,6 +94,7 @@
 LINE = 4
 LANES = 128
 PARTS = 2
+SENT_BY = {1: 1, 2: 2, 3: 3, 13: 3, 5: 4, 14: 4}
 FIRST_AT = (9.6, 11.3, 14.5, 16.8)
 RELAY_AT = (5.65, 8.45, 11.25, 12.4)
 CROSS_IN = (-5.5, -5.4, -2.6, -1.9)
@@ -143,7 +144,7 @@
 
     def copy_to(src, dst, stage, sems, where, peer):
         return pltpu.make_async_remote_copy(
-            src_ref=src, dst_ref=dst, send_sem=out_sem.at[stage],
+            src_ref=src, dst_ref=dst, send_sem=out_sem.at[SENT_BY.get(stage, 0)],
             recv_sem=sems.at[where], device_id=peer, device_id_type=MESH,
         )
 
@@ -210,7 +211,6 @@
                 place[span, at] = (row == line + base).astype(f32).astype(bf16)
 
     smalls[0].wait()
-    one_hots(ids_ref, 0, pick_own, place_own, 0)
 
     pl.semaphore_wait(barrier, 8 + 2 * is_inner.astype(jnp.int32))
 
@@ -258,6 +258,7 @@
                 block_send(j, 0)
 
     def stage_ids():
+        one_hots(ids_ref, 0, pick_own, place_own, 0)
         ids_x.wait_recv()
         one_hots(ids_all.at[1], 1, pick_own, place_own, 0)
 
@@ -275,6 +276,9 @@
         at = pl.ds(pl.multiple_of(of_dat * cap_dev, cap_dev), cap_dev)
         return rows.at[feature, pair(p), at]
 
+    def late_at(k, p):
+        return (k + p if k == last else k,)
+
     def dat_at(of_dat):
         return pl.ds(pl.multiple_of(of_dat * cap_dev, cap_dev), cap_dev)
 
@@ -299,14 +303,15 @@
 
     def c_copy(k, rel, p, of_dat):
         ref = own_rows(k, rel, p, of_dat)
-        return copy_to(ref, ref, 8, c_sem, (k, p), c_peer)
+        return copy_to(ref, ref, 8, c_sem, late_at(k, p), c_peer)
 
     def relay_copy(k, rel, p, of_dat):
         ref = own_rows(k, rel, p, of_dat)
-        return copy_to(ref, ref, 9, cr_sem, (k, p), c_peer)
+        return copy_to(ref, ref, 9, cr_sem, late_at(k, p), c_peer)
 
     def both_rows(k, p, of_dat):
-        return rows.at[k * PAIR : (k + 1) * PAIR, pair(p), dat_at(of_dat)]
+        parts_at = pair(p) if k == last else slice(0, experts_dev)
+        return rows.at[k * PAIR : (k + 1) * PAIR, parts_at, dat_at(of_dat)]
 
     dat_y = dat + PAIR - 2 * PAIR * y
     dat_c = dat + 1 - 2 * c
@@ -381,8 +386,9 @@
 
     def stage_first(k, p):
         for sems, stage, of_dat in ((c_sem, 8, dat_c), (cr_sem, 9, dat_yc)):
-            ref = both_rows(k, p, of_dat)
-            copy_to(ref, ref, stage, sems, (k, p), c_peer).wait_recv()
+            if k == last or p == 0:
+                ref = both_rows(k, p, of_dat)
+                copy_to(ref, ref, stage, sems, late_at(k, p), c_peer).wait_recv()
         if k == 0 and p == 0:
             inner_load.wait()
 
@@ -405,7 +411,7 @@
         return copy_to(y_send.at[k, pair(p)], y_recv.at[k, pair(p)], 11, ry_sem, (k, p), y_peer)
 
     def back_x(k, p):
-        return copy_to(give.at[k, pair(p)], slots_v.at[k, 1, pair(p)], 12, rx_sem, (k, p), x_peer)
+        return copy_to(give.at[k, pair(p)], slots_v.at[k, 1, pair(p)], 12, rx_sem, (k,), x_peer)
 
     def raw_copy(k, xr, p):
         return copy_to(
@@ -460,8 +466,9 @@
         slots_v[k, 0, pair(p)] = own.astype(bf16)
         send(raw_copy(k, 0, p), is_end)
 
-    def stage_cross(k, p):
-        back_x(k, p).wait_recv()
+    def stage_cross(k):
+        ref = slots_v.at[k, 1]
+        copy_to(ref, ref, 12, rx_sem, (k,), x_peer).wait_recv()
 
     def dest_out(k, j, total, peer, peer_diag):
         for xr in (1, 0):
@@ -586,8 +593,7 @@
         order += [
             (2 * k + 0.0, stage_weigh, (k, 0)),
             (2 * k + 1.0, stage_weigh, (k, 1)),
-            (2 * k + 2.1, stage_cross, (k, 0)),
-            (2 * k + 3.1, stage_cross, (k, 1)),
+            (2 * k + 3.1, stage_cross, (k,)),
             (2 * k + 3.2, stage_place, (k,)),
             (2 * k + 6.05, stage_far, (k,)),
             (2 * k + 11.4, stage_total, (k,)),
@@ -596,6 +602,15 @@
     for _, stage, where in sorted(order, key=lambda step: step[0]):
         stage(*where)
 
+    def count(*refs):
+        total = 0
+        for ref in refs:
+            size = 1
+            for extent in ref.shape:
+                size *= extent
+            total += size
+        return total
+
     def sent(ref, stage, cond=None):
         done = copy_to(ref, ref, stage, ids_sem, (0,), x_peer)
         if cond is None:
@@ -603,22 +618,24 @@
         else:
             pl.when(cond)(done.wait_send)
 
+    width, units = inner_v.shape[1], inner_v.shape[2]
+
+    def sized(total):
+        whole_e, lines = divmod(total, width * units)
+        if lines == 0:
+            return outer_v.at[0:whole_e]
+        assert whole_e == 0 and lines % width == 0
+        return outer_v.at[0, 0 : lines // width]
+
     own_all = rows.at[:, :, dat_at(dat)]
-    sent(cross, 0)
+    half_parts = parts.at[:, :, 1 - c]
+    always = count(cross, blocks.at[0], swap_send, own_all, own_all, own_all, half_parts)
+    always += count(y_send, give, last_send)
+    sent(sized(always), 0)
     sent(ids_ref, 1)
     sent(ids_all.at[2:4], 2, is_end)
-    sent(blocks.at[0], 3, is_end)
-    sent(blocks.at[0], 4)
-    sent(pick_send, 5, is_inner)
-    sent(swap_send, 6)
-    for stage in (7, 8, 9):
-        sent(own_all, stage)
-    sent(parts.at[:, :, 1 - c], 10)
-    sent(y_send, 11)
-    sent(give, 12)
-    sent(slots_v, 13, is_end)
-    sent(dest_send, 14, is_inner)
-    sent(last_send, 15)
+    sent(sized(count(blocks.at[0], slots_v)), 3, is_end)
+    sent(sized(count(pick_send, dest_send)), 5, is_inner)
 
 
 def kernel_body(tokens, norm_gain, router_weight, inner_weight, outer_weight, slot_tokens, slot_ids):
@@ -680,7 +697,7 @@
             buffer(chunks, tok_rows, LANES),
             buffer(chunks, tok_rows, LANES, kind=f32),
             dma((6,)),
-            dma((16,)),
+            dma((5,)),
             dma((2,)),
             dma((chunks,)),
             dma((chunks,)),
@@ -688,11 +705,11 @@
             dma((chunks, PAIR, PARTS)),
             dma((chunks, PARTS)),
             dma((chunks, PAIR, PARTS)),
+            dma((chunks - 1 + PARTS,)),
+            dma((chunks - 1 + PARTS,)),
             dma((chunks, PARTS)),
             dma((chunks, PARTS)),
-            dma((chunks, PARTS)),
-            dma((chunks, PARTS)),
-            dma((chunks, PARTS)),
+            dma((chunks,)),
             dma((chunks,)),
             dma((chunks, PAIR)),
             dma((chunks,)),

time: 56.8 us -> 56.6 us (level)
  no operation moved by 1% of the time
where the time goes in v5:
time: 56.6 us; the launch traced here: 56.4 us
  Pallas kernels  55.7 us (98%)
  local copies, waits for them, and re-layouts  0.71 us (1%)
    pallas_call x1, Pallas kernels, kernel_body(): pl.pallas_call(moe_kernel, out_shape=jax.ShapeDtypeStruct((tok_rows, widt...  55.7 us

profile of v5, /device:TPU:0, one launch (start us, length us, event | category | flops | bytes accessed | tf_op | source)
XLA Modules:
  0.0 56.4 jit_solution(4632637777597200862)
XLA Ops:
  0.0 55.7 %shard_map.64 = bf16[128,1024]{1,0:T(8,128)(2,1)S(1)} custom-call(bf16[128,1024]{1,0:T(8,128)(2,1)} %tokens_hbm.1, f32[1,1024]{1,0:T(1,128)} %bitcast.3, bf16[4,1024]{1,0:T(4,128)(2,1)} %bitcast.2, s32[4,64]{1,0:T(4,128)} %ids_hbm.1, bf16[4,1024,1024]{2,1,0:T(8,128)(2,1)} %inner_hbm.1, bf16[4,1024,1024]{2,1,0:T(8,128)(2,1)} %outer_hbm.1), custom_call_target="tpu_custom_call" | custom-call | tf_op jit(solution)/shard_map/pallas_call | solution.py:659
  55.7 0.7 %copy.8 = bf16[128,1024]{1,0:T(8,128)(2,1)} copy(bf16[128,1024]{1,0:T(8,128)(2,1)S(1)} %shard_map.64) | data formatting | bytes 524288

commit v6 on v5

--- a/solution.py
+++ b/solution.py
@@ -473,7 +473,8 @@
     def dest_out(k, j, total, peer, peer_diag):
         for xr in (1, 0):
             dest_send[k, j, xr] = total[xr * tok_rows : (xr + 1) * tok_rows].astype(bf16)
-            dest_copy(k, j, xr, peer_diag if k == last and xr == 1 else peer).start()
+            if (k, j, xr) != (last - 1, 1, 0):
+                dest_copy(k, j, xr, peer_diag if k == last and xr == 1 else peer).start()
 
     def last_out(k, total):
         last_send[k] = total.astype(bf16)
@@ -504,6 +505,8 @@
             ends = raw[k].reshape(PAIR * slots, LANES)
             theirs = jnp.dot(place_far[2 * both :, :], ends, preferred_element_type=f32)
             dest_out(k, 2, mine[both:] + theirs, far_end, far_end_diag)
+            if k == last:
+                dest_copy(k - 1, 1, 0, far_inner).start()
             theirs = jnp.dot(place_far[both : 2 * both, :], ends, preferred_element_type=f32)
             dest_out(k, 1, mine[:both] + theirs, far_inner, far_diag)
             total = dense[k] + jnp.dot(place_far[:both, :], ends, preferred_element_type=f32)

time: 56.6 us -> 56.5 us (level)
  no operation moved by 1% of the time
where the time goes in v6:
time: 56.5 us; the launch traced here: 56.4 us
  Pallas kernels  55.6 us (98%)
  local copies, waits for them, and re-layouts  0.71 us (1%)
    pallas_call x1, Pallas kernels, kernel_body(): pl.pallas_call(moe_kernel, out_shape=jax.ShapeDtypeStruct((tok_rows, widt...  55.6 us

profile of v6, /device:TPU:0, one launch (start us, length us, event | category | flops | bytes accessed | tf_op | source)
XLA Modules:
  0.0 56.4 jit_solution(6278675034459432456)
XLA Ops:
  0.0 55.6 %shard_map.64 = bf16[128,1024]{1,0:T(8,128)(2,1)S(1)} custom-call(bf16[128,1024]{1,0:T(8,128)(2,1)} %tokens_hbm.1, f32[1,1024]{1,0:T(1,128)} %bitcast.3, bf16[4,1024]{1,0:T(4,128)(2,1)} %bitcast.2, s32[4,64]{1,0:T(4,128)} %ids_hbm.1, bf16[4,1024,1024]{2,1,0:T(8,128)(2,1)} %inner_hbm.1, bf16[4,1024,1024]{2,1,0:T(8,128)(2,1)} %outer_hbm.1), custom_call_target="tpu_custom_call" | custom-call | tf_op jit(solution)/shard_map/pallas_call | solution.py:662
  55.6 0.7 %copy.8 = bf16[128,1024]{1,0:T(8,128)(2,1)} copy(bf16[128,1024]{1,0:T(8,128)(2,1)S(1)} %shard_map.64) | data formatting | bytes 524288
